TPU v7x, 32 devices: a whole 2x2x4 slice. The times are simulated.
32 devices in a mesh: gx: 4 (over x, core), gy: 4 (over z), gz: 2 (over y).
Axes of the slice: x: 2, y: 2, z: 4, core: 2. Of those that a mesh axis runs over, the one named last changes fastest.
Arguments:
- points: float32 [16384, 768], P(('gx', 'gy', 'gz')), may hold values from -6 to 6
- assignment: int32 [16384], P(('gx', 'gy', 'gz')), may hold values from 0 to 32767, as said below
- sample_index: int32 [16384], P(('gx', 'gy', 'gz')), may hold values from 0 to 511
Outputs:
- means: float32 [32768, 768], P(('gx', 'gy', 'gz'))
- centroids: float32 [32768, 768], P(('gx', 'gy', 'gz'))
Inputs may be any that keep to these rules, and one draw needn't show every extreme that they name: `assignment`: among the 512 points of one aligned block, at most 32 have a cluster in any one range of 1024 consecutive cluster numbers that starts at a multiple of 1024; in every block some range holds exactly 32.
All inputs are finite; a program needn't handle non-finite values.
Results may differ from a plain program's by a relative error of at most 0.00007.
Values sent between devices are 32-bit elements; how exact they have to be, the bound alone decides.
No kernel may reach another device: no remote copies, remote signals or barrier semaphores. Data moves between devices by JAX's collectives and lax.ppermute only.
A program may use at most 64 MiB of HBM per device.

v0:
```python
import math

import jax
import jax.numpy as jnp
from jax import lax
from jax.sharding import PartitionSpec as P

CL_DEV = 1024


def body(points, assignment, sample_index):
    count_pts, features = points.shape
    size_gx = lax.axis_size("gx")
    rest = lax.axis_size("gy") * lax.axis_size("gz")
    devices = size_gx * rest
    capacity = 2 * count_pts // devices
    point_ids = jnp.arange(count_pts, dtype=jnp.int32)
    weight = jnp.zeros((count_pts,), jnp.float32).at[sample_index].add(1.0)
    owner = assignment // CL_DEV
    inside = assignment - owner * CL_DEV
    owner_hot = (owner[:, None] == jnp.arange(devices, dtype=jnp.int32)[None, :]).astype(
        jnp.float32
    )
    earlier = (point_ids[:, None] > point_ids[None, :]).astype(jnp.float32)
    before = jnp.dot(earlier, owner_hot, precision=lax.Precision.HIGHEST)
    place = jnp.sum(before * owner_hot, axis=1).astype(jnp.int32)
    slot = owner * capacity + place
    source = jnp.zeros((devices * capacity,), jnp.int32).at[slot].set(point_ids)
    filled = jnp.zeros((devices * capacity,), jnp.float32).at[slot].set(weight)
    tags = jnp.zeros((devices * capacity,), jnp.float32).at[slot].set(inside.astype(jnp.float32))
    rows = jnp.take(points, source, axis=0)
    got_rows, got_weight, got_tags = (
        lax.all_to_all(
            rows.reshape(devices, capacity, features),
            ("gx", "gy", "gz"),
            split_axis=0,
            concat_axis=0,
            tiled=True,
        ),
        lax.all_to_all(
            filled.reshape(devices, capacity),
            ("gx", "gy", "gz"),
            split_axis=0,
            concat_axis=0,
            tiled=True,
        ),
        lax.all_to_all(
            tags.reshape(devices, capacity),
            ("gx", "gy", "gz"),
            split_axis=0,
            concat_axis=0,
            tiled=True,
        ),
    )
    received = devices * capacity
    got_rows = got_rows.reshape(received, features)
    got_weight = got_weight.reshape(received)
    got_tags = got_tags.reshape(received)
    block_rows = math.gcd(received, 512)
    block_count = received // block_rows
    cluster_ids = jnp.arange(CL_DEV, dtype=jnp.float32)

    def accumulate(carry, index):
        totals, tally = carry
        start = index * block_rows
        rows_b = lax.dynamic_slice_in_dim(got_rows, start, block_rows, 0)
        weight_b = lax.dynamic_slice_in_dim(got_weight, start, block_rows, 0)
        tags_b = lax.dynamic_slice_in_dim(got_tags, start, block_rows, 0)
        onehot = (tags_b[:, None] == cluster_ids[None, :]).astype(jnp.float32) * weight_b[:, None]
        totals = totals + jnp.einsum("rk,rd->kd", onehot, rows_b, precision=lax.Precision.HIGHEST)
        tally = tally + jnp.sum(onehot, axis=0)
        return ((totals, tally), None)

    start_carry = (jnp.zeros((CL_DEV, features), jnp.float32), jnp.zeros((CL_DEV,), jnp.float32))
    (owned, owned_tally), unused = lax.scan(
        accumulate, start_carry, jnp.arange(block_count, dtype=jnp.int32)
    )
    means = owned / jnp.maximum(owned_tally, 1.0)[:, None]
    centroids = means / jnp.sqrt(jnp.sum(means * means, axis=1, keepdims=True) + 1e-06)
    return (means, centroids)


def solution(mesh):
    return jax.shard_map(
        body,
        mesh=mesh,
        in_specs=(P(("gx", "gy", "gz"), None), P(("gx", "gy", "gz")), P(("gx", "gy", "gz"))),
        out_specs=(P(("gx", "gy", "gz"), None), P(("gx", "gy", "gz"), None)),
        check_vma=False,
    )
```

profile of v0, /device:TPU:0, one launch (start us, length us, event | category | flops | bytes accessed | tf_op | source)
XLA Modules:
  0.0 144.5 jit_solution(2040249376559193315)
XLA Ops:
  0.6 0.8 subtract_convert_fusion
  1.7 2.4 %scatter_custom_fusion = f32[1024]{0:T(1024)S(1)} fusion(s32[512]{0:T(512)S(1)} %compare_select_fusion.2, f32[512]{0:T(512)S(1)} %get-tuple-element.89, f32[]{:T(128)} %constant.32.clone.1), kind=kCustom, calls=%fused_computation.45 | custom fusion | bytes 4100 | tf_op jit(solution)/shard_map/scatter | solution.py:30
  4.2 0.7 all_to_all.15
  4.9 7.3 %all-to-all-start = ((f32[32,1,32]{2,1,0:T(1,128)}), f32[32,1,32]{2,1,0:T(1,128)S(1)}, u32[]{:S(2)}, u32[]{:S(2)}) async-start(f32[32,1,32]{2,1,0:T(1,128)} %all_to_all.15), calls=%async_computation | async-start | bytes 32768 | tf_op jit(solution)/shard_map/all_to_all | solution.py:47
  12.2 2.4 %scatter_custom_fusion.3 = s32[1024]{0:T(1024)S(1)} fusion(s32[512]{0:T(512)S(1)} %compare_select_fusion.2, s32[512]{0:T(512)S(1)} %iota.21, s32[]{:T(128)} %constant.31.clone.1), kind=kCustom, calls=%fused_computation.39 | custom fusion | bytes 4100 | tf_op jit(solution)/shard_map/scatter | solution.py:28
  14.7 0.7 compare_select_fusion.1
  15.4 4.1 %scatter_custom_fusion.1 = f32[512]{0:T(512)S(1)} fusion(s32[512]{0:T(512)S(1)} %compare_select_fusion.1, f32[512]{0:T(512)S(1)} %broadcast.37, f32[]{:T(128)} %constant.32.clone.1), kind=kCustom, calls=%fused_computation.48 | custom fusion | flops 512 | bytes 2052 | tf_op jit(solution)/shard_map/scatter-add | solution.py:18
  19.5 2.4 %scatter_custom_fusion.2 = f32[1024]{0:T(1024)S(1)} fusion(s32[512]{0:T(512)S(1)} %compare_select_fusion.2, f32[512]{0:T(512)S(1)} %scatter_custom_fusion.1, f32[]{:T(128)} %constant.32.clone.1), kind=kCustom, calls=%fused_computation.43 | custom fusion | bytes 4100 | tf_op jit(solution)/shard_map/scatter | solution.py:29
  22.0 0.7 all_to_all.17
  22.7 5.2 %gather_fusion = f32[1024,768]{1,0:T(8,128)} fusion(f32[512,768]{1,0:T(8,128)S(1)} %copy-done, s32[1024]{0:T(1024)S(1)} %fusion.14), kind=kCustom, calls=%fused_computation | custom fusion | bytes 6295552 | tf_op jit(solution)/shard_map/jit(_take)/gather | solution.py:31
  27.9 5.8 %all-to-all-start.1 = ((f32[32,1,32]{2,1,0:T(1,128)}), f32[32,1,32]{2,1,0:T(1,128)S(1)}, u32[]{:S(2)}, u32[]{:S(2)}) async-start(f32[32,1,32]{2,1,0:T(1,128)} %all_to_all.17), calls=%async_computation.1 | async-start | bytes 32768 | tf_op jit(solution)/shard_map/all_to_all | solution.py:40
  33.8 3.9 %broadcast_select_fusion = f32[32,32,768]{2,1,0:T(8,128)} fusion(f32[32,32,768]{2,1,0:T(8,128)} %bitcast.8, pred[32,32]{1,0:T(8,128)(4,1)S(1)} %broadcast_in_dim.49), kind=kLoop, calls=%fused_computation.21 | loop fusion | flops 786432 | bytes 6292480 | tf_op jit(solution)/shard_map/jit(_take)/select_n | solution.py:31
  37.6 3.3 %all-to-all-done.1 = f32[32,1,32]{2,1,0:T(1,128)S(1)} async-done(((f32[32,1,32]{2,1,0:T(1,128)}), f32[32,1,32]{2,1,0:T(1,128)S(1)}, u32[]{:S(2)}, u32[]{:S(2)}) %all-to-all-start.1) | async-done | bytes 4128 | tf_op jit(solution)/shard_map/all_to_all | solution.py:40
  40.9 3.5 %all-to-all-start.2 = ((f32[32,32,768]{2,1,0:T(8,128)}), f32[32,32,768]{2,1,0:T(8,128)}, u32[]{:S(2)}, u32[]{:S(2)}) async-start(f32[32,32,768]{2,1,0:T(8,128)} %broadcast_select_fusion), calls=%async_computation.2 | async-start | bytes 6291456 | tf_op jit(solution)/shard_map/all_to_all | solution.py:33
  45.0 0.7 reduce.6
  45.7 0.7 reduce.7
  46.5 71.0 %all-to-all-done.2 = f32[32,32,768]{2,1,0:T(8,128)} async-done(((f32[32,32,768]{2,1,0:T(8,128)}), f32[32,32,768]{2,1,0:T(8,128)}, u32[]{:S(2)}, u32[]{:S(2)}) %all-to-all-start.2) | async-done | bytes 3145760 | tf_op jit(solution)/shard_map/all_to_all | solution.py:33
  117.4 21.0 %while.13 = (s32[]{:T(128)}, f32[1024,768]{1,0:T(8,128)}, f32[1024]{0:T(1024)S(1)}, s32[2]{0:T(128)S(1)}, f32[1024]{0:T(1024)S(1)}, /*index=5*/f32[1024]{0:T(102...) while((s32[]{:T(128)}, f32[1024,768]{1,0:T(8,128)}, ...), condition=%wide.region_7.8_spmd.clone, body=%wide.region_5.7_spmd.clone.sunk | while | flops 4836033536 | bytes 7897286 | solution.py:75
  117.4 0.6 dynamic_slice.24
  119.1 8.6 %select_add_fusion.4 = f32[1024,768]{1,0:T(8,128)} fusion(f32[1024,768]{1,0:T(8,128)} %get-tuple-element.146, f32[1024,768]{1,0:T(8,128)} %get-tuple-element.162, s32[]{:T(128)S(6)} %select_n.45, pred[]{:T(512)S(6)} %compare.5, f32[512]{0:T(512)S(1)} %dynamic_slice.25, f32[512]{0:T(512)S(1)} %dynamic_slice.26), kind=kOutput, calls=%fused_computation.6.clone.1 | convolution fusion | flops 4834459648 | bytes 7868421 | tf_op jit(solution)/shard_map/while/body/eval_jaxpr/rk,rd->kd/dot_general | solution.py:70
  127.7 0.6 dynamic_slice.24
  129.4 9.0 %select_add_fusion.4 = f32[1024,768]{1,0:T(8,128)} fusion(f32[1024,768]{1,0:T(8,128)} %get-tuple-element.146, f32[1024,768]{1,0:T(8,128)} %get-tuple-element.162, s32[]{:T(128)S(6)} %select_n.45, pred[]{:T(512)S(6)} %compare.5, f32[512]{0:T(512)S(1)} %dynamic_slice.25, f32[512]{0:T(512)S(1)} %dynamic_slice.26), kind=kOutput, calls=%fused_computation.6.clone.1 | convolution fusion | flops 4834459648 | bytes 7868421 | tf_op jit(solution)/shard_map/while/body/eval_jaxpr/rk,rd->kd/dot_general | solution.py:70
  138.4 4.1 %multiply_reduce_fusion = (f32[1024]{0:T(1024)S(1)}, f32[1024,768]{1,0:T(8,128)}) fusion(f32[1024,768]{1,0:T(8,128)} %get-tuple-element.45, f32[1024]{0:T(1024)S(1)} %broadcast_maximum_fusion), kind=kLoop, calls=%fused_computation.18 | loop fusion | flops 2358272 | bytes 6299648 | tf_op jit(solution)/shard_map/reduce_sum | solution.py:79
  142.5 1.9 %broadcast_divide_fusion = f32[1024,768]{1,0:T(8,128)} fusion(f32[1024,768]{1,0:T(8,128)S(1)} %copy-done.1, f32[1024]{0:T(1024)S(1)} %sqrt_multiply_fusion), kind=kLoop, calls=%fused_computation.19 | loop fusion | flops 786432 | bytes 6295552 | tf_op jit(solution)/shard_map/div | solution.py:79
  (28 shorter events, 2.0 us)
Async XLA Ops:
  0.6 22.1 %copy-start = (f32[512,768]{1,0:T(8,128)S(1)}, f32[512,768]{1,0:T(8,128)}, u32[]{:S(2)}) copy-start(f32[512,768]{1,0:T(8,128)} %param.5) | copy-start | bytes 4718596
  4.9 23.0 %all-to-all-start = ((f32[32,1,32]{2,1,0:T(1,128)}), f32[32,1,32]{2,1,0:T(1,128)S(1)}, u32[]{:S(2)}, u32[]{:S(2)}) async-start(f32[32,1,32]{2,1,0:T(1,128)} %all_to_all.15), calls=%async_computation | async-start | bytes 32768 | tf_op jit(solution)/shard_map/all_to_all | solution.py:47
  27.9 13.0 %all-to-all-start.1 = ((f32[32,1,32]{2,1,0:T(1,128)}), f32[32,1,32]{2,1,0:T(1,128)S(1)}, u32[]{:S(2)}, u32[]{:S(2)}) async-start(f32[32,1,32]{2,1,0:T(1,128)} %all_to_all.17), calls=%async_computation.1 | async-start | bytes 32768 | tf_op jit(solution)/shard_map/all_to_all | solution.py:40
  40.9 76.5 %all-to-all-start.2 = ((f32[32,32,768]{2,1,0:T(8,128)}), f32[32,32,768]{2,1,0:T(8,128)}, u32[]{:S(2)}, u32[]{:S(2)}) async-start(f32[32,32,768]{2,1,0:T(8,128)} %broadcast_select_fusion), calls=%async_computation.2 | async-start | bytes 6291456 | tf_op jit(solution)/shard_map/all_to_all | solution.py:33
  138.4 4.1 %copy-start.1 = (f32[1024,768]{1,0:T(8,128)S(1)}, f32[1024,768]{1,0:T(8,128)}, u32[]{:S(2)}) copy-start(f32[1024,768]{1,0:T(8,128)} %get-tuple-element.45) | copy-start | bytes 9437188
where the time goes:
time: 145 us; the launch traced here: 144 us
  waiting for transfers between devices  74.3 us (51%)
  matrix products  17.8 us (12%)
  other arithmetic  17.4 us (12%)
  starting transfers between devices  16.7 us (12%)
  local copies, waits for them, and re-layouts  16.2 us (11%)
    all_to_all x1, waiting for transfers between devices, body(): lax.all_to_all(rows.reshape(devices, capacity, features), ('gx', 'gy', 'g...  71 us
    dot_general x2, matrix products, accumulate(): jnp.einsum('rk,rd->kd', onehot, rows_b, precision=lax.Precision.HIGHEST)  17.6 us
    all_to_all x1, starting transfers between devices, body(): lax.all_to_all(tags.reshape(devices, capacity), ('gx', 'gy', 'gz'), split...  7.33 us
    all_to_all x1, starting transfers between devices, body(): lax.all_to_all(filled.reshape(devices, capacity), ('gx', 'gy', 'gz'), spl...  5.83 us
    gather x1, local copies, waits for them, and re-layouts, body(): rows = jnp.take(points, source, axis=0)  5.22 us
    reduce_sum x1, other arithmetic, body(): jnp.sum(means * means, axis=1, keepdims=True) + 1e-06  4.13 us
    scatter-add x1, other arithmetic, body(): weight = jnp.zeros((count_pts,), jnp.float32).at[sample_index].add(1.0)  4.08 us
    select_n x1, other arithmetic, body(): rows = jnp.take(points, source, axis=0)  3.85 us
  transfers between devices with their start and end apart: 3, of which 2 were waited for; matrix products, arithmetic and copies ran while one was open for 14% of the time, Pallas kernels for 0%

commit v1 on v0

--- a/solution.py
+++ b/solution.py
@@ -1,14 +1,21 @@
+import functools
 import math
 
 import jax
 import jax.numpy as jnp
 from jax import lax
+from jax.experimental import pallas as pl
+from jax.experimental.pallas import tpu as pltpu
 from jax.sharding import PartitionSpec as P
 
 CL_DEV = 1024
-
-
-def body(points, assignment, sample_index):
+LANES = 128
+F32 = jnp.float32
+BF16 = jnp.bfloat16
+I32 = jnp.int32
+
+
+def full_body(points, assignment, sample_index):
     count_pts, features = points.shape
     size_gx = lax.axis_size("gx")
     rest = lax.axis_size("gy") * lax.axis_size("gz")
@@ -80,6 +87,301 @@
     return (means, centroids)
 
 
+def shift_div(x, n):
+    return lax.shift_right_logical(x, jnp.int32(n.bit_length() - 1))
+
+
+def iota(shape, dim):
+    return lax.broadcasted_iota(I32, shape, dim)
+
+
+def as_bf16(mask):
+    return jnp.where(mask, 1.0, 0.0).astype(BF16)
+
+
+def nt_dot(a, b):
+    return lax.dot_general(a, b, (((1,), (1,)), ((), ())), preferred_element_type=F32)
+
+
+def nn_dot(a, b):
+    return jnp.dot(a, b, preferred_element_type=F32)
+
+
+def three(x):
+    hi = x.astype(BF16)
+    rest = x - hi.astype(F32)
+    mid = rest.astype(BF16)
+    low = (rest - mid.astype(F32)).astype(BF16)
+    return hi, mid, low
+
+
+def place(hot, group, chunks, room):
+    groups = hot.shape[0]
+    upper = as_bf16(iota((LANES, LANES), 0) < iota((LANES, LANES), 1))
+    run = jnp.zeros((groups, 1), F32)
+    places = []
+    for c in range(chunks):
+        h = hot[:, c * LANES : (c + 1) * LANES]
+        before = nn_dot(h.astype(BF16), upper) + run
+        places.append(jnp.sum(before * h, axis=0, keepdims=True))
+        run = run + jnp.sum(h, axis=1, keepdims=True)
+    return jnp.concatenate(places, axis=1), jnp.max(run)
+
+
+def pack(x3, ids, weight, valid, group, groups, room, flag, chunks, write):
+    lanes = chunks * LANES
+    hot = jnp.where((iota((groups, lanes), 0) == group) & valid, 1.0, 0.0)
+    pos, most = place(hot, group, chunks, room)
+    over = jnp.where(most > room - 1, 1.0, 0.0)
+    flag = jnp.maximum(flag, over)
+    pos = pos.astype(I32)
+    keep = valid & (pos < room - 1)
+    slot = jnp.where(keep, group * room + pos, -1)
+    pick = as_bf16(iota((groups * room, lanes), 0) == slot)
+    out = nn_dot(pick, x3[0]) + nn_dot(pick, x3[1]) + nn_dot(pick, x3[2])
+    tag_slot = jnp.where(keep, group * LANES + pos, -1)
+    pick_tag = as_bf16(iota((groups * LANES, lanes), 0) == tag_slot)
+    w = weight.astype(I32)
+    parts = [
+        shift_div(ids, 16384),
+        shift_div(ids, 128) & 127,
+        ids & 127,
+        shift_div(w, 128),
+        w & 127,
+    ]
+    row = iota((8, lanes), 0)
+    stack = jnp.zeros((8, lanes), F32)
+    for k, part in enumerate(parts):
+        stack = jnp.where(row == k, part.astype(F32), stack)
+    tags = nt_dot(stack.astype(BF16), pick_tag)
+    tag_ids = tags[0:1] * 16384.0 + tags[1:2] * 128.0 + tags[2:3]
+    tag_w = tags[3:4] * 128.0 + tags[4:5]
+    flags = jnp.full((1, LANES), 1.0, F32) * flag
+    for g in range(groups):
+        write(
+            g,
+            out[g * room : (g + 1) * room],
+            tag_ids[:, g * LANES : (g + 1) * LANES],
+            tag_w[:, g * LANES : (g + 1) * LANES],
+            flags,
+        )
+    return flag
+
+
+def write_block(ref, at, room, rows, tag_ids, tag_w, flags):
+    ref[at + (slice(0, room), slice(None))] = rows
+    last = slice(room - 1, room)
+    ref[at + (last, slice(0, LANES))] = tag_ids
+    ref[at + (last, slice(LANES, 2 * LANES))] = tag_w
+    ref[at + (last, slice(2 * LANES, 3 * LANES))] = flags
+
+
+def split_owner(ids, sizes):
+    n_gx, n_gy, n_gz = sizes
+    owner = shift_div(ids, CL_DEV)
+    gz = owner & (n_gz - 1)
+    gy = shift_div(owner, n_gz) & (n_gy - 1)
+    gx = shift_div(owner, n_gz * n_gy)
+    return gy, gx * n_gz + gz
+
+
+def prepare_kernel(sizes, rooms, my_ref, points_ref, assign_ref, index_ref, *outs):
+    n_gx, n_gy, n_gz = sizes
+    room_a, room_b = rooms
+    a_refs, b_ref = outs[:n_gy], outs[n_gy]
+    count_pts = points_ref.shape[0]
+    half = points_ref.shape[1] // 2
+    chunks = count_pts // LANES
+    ids = assign_ref[...]
+    hot = as_bf16(iota((count_pts, count_pts), 0) == index_ref[...])
+    weight = nt_dot(jnp.ones((8, count_pts), BF16), hot)[0:1]
+    weight_col = nn_dot(hot, jnp.ones((count_pts, LANES), BF16))
+    valid = weight > 0.0
+    wide = jnp.concatenate([weight_col] * (half // LANES), axis=1)
+    gy, plane = split_owner(ids, sizes)
+    shift = (gy - my_ref[0] + n_gy) & (n_gy - 1)
+    pack(
+        three(points_ref[:, :half] * wide), ids, weight, valid, shift, n_gy, room_a, jnp.float32(0.0),
+        chunks, lambda g, *v: write_block(a_refs[g], (), room_a, *v),
+    )
+    pack(
+        three(points_ref[:, half:] * wide), ids, weight, valid, plane, n_gx * n_gz, room_b,
+        jnp.float32(0.0), chunks, lambda g, *v: write_block(b_ref, (g,), room_b, *v),
+    )
+
+
+def gathered(blocks):
+    rows, ids, weight, flag = [], [], [], jnp.zeros((1, LANES), F32)
+    for block in blocks:
+        room, width = block.shape
+        rows.append(block)
+        if room < LANES:
+            rows.append(jnp.zeros((LANES - room, width), F32))
+        last = block[room - 1 : room]
+        ids.append(last[:, :LANES])
+        weight.append(last[:, LANES : 2 * LANES])
+        flag = jnp.maximum(flag, last[:, 2 * LANES : 3 * LANES])
+    return (
+        jnp.concatenate(rows, axis=0),
+        jnp.concatenate(ids, axis=1).astype(I32),
+        jnp.concatenate(weight, axis=1),
+        jnp.max(flag),
+    )
+
+
+def forward_kernel(sizes, rooms, my_ref, *refs):
+    n_gx, n_gy, n_gz = sizes
+    room_a, room_b = rooms
+    n_plane = n_gx * n_gz
+    a_in, b_in = refs[:n_gy], refs[n_gy]
+    a_out, b_out = refs[n_gy + 1], refs[n_gy + 2 : 2 * n_gy + 2]
+    rows_a, ids_a, weight_a, flag_a = gathered([r[...] for r in a_in])
+    rows_b, ids_b, weight_b, flag_b = gathered([b_in[g] for g in range(n_plane)])
+    flag = jnp.maximum(flag_a, flag_b)
+    gy_b, unused = split_owner(ids_b, sizes)
+    unused, plane_a = split_owner(ids_a, sizes)
+    shift = (gy_b - my_ref[0] + n_gy) & (n_gy - 1)
+    flag = pack(
+        three(rows_b), ids_b, weight_b, weight_b > 0.0, shift, n_gy, room_b, flag, n_plane,
+        lambda g, *v: write_block(b_out[g], (), room_b, *v),
+    )
+    pack(
+        three(rows_a), ids_a, weight_a, weight_a > 0.0, plane_a, n_plane, room_a, flag, n_gy,
+        lambda g, *v: write_block(a_out, (g,), room_a, *v),
+    )
+
+
+def finish_kernel(sizes, steps, my_ref, *refs):
+    n_gx, n_gy, n_gz = sizes
+    n_plane = n_gx * n_gz
+    a_in, b_in = refs[0], refs[1 : n_gy + 1]
+    means_ref, cent_ref = refs[n_gy + 1 : n_gy + 3]
+    xa, xb, ta, tb = refs[n_gy + 3 :]
+    block = means_ref.shape[0]
+    half = means_ref.shape[1] // 2
+    step = pl.program_id(0)
+
+    @pl.when(step == 0)
+    def _():
+        base = my_ref[0] * CL_DEV
+        for source, x, t in (
+            ([a_in[g] for g in range(n_plane)], xa, ta),
+            ([r[...] for r in b_in], xb, tb),
+        ):
+            rows, ids, weight, unused = gathered(source)
+            for k, part in enumerate(three(rows)):
+                x[k] = part
+            w = weight.astype(I32)
+            t[0:1, :] = jnp.where(w > 0, ids - base, -1)
+            t[1:2, :] = w
+
+    first = step * block
+    totals = []
+    for x, t in ((xa, ta), (xb, tb)):
+        lanes = t.shape[1]
+        hot = as_bf16(iota((block, lanes), 0) + first == t[0:1, :])
+        totals.append(nn_dot(hot, x[0]) + nn_dot(hot, x[1]) + nn_dot(hot, x[2]))
+    w = tb[1:2, :]
+    lanes = tb.shape[1]
+    high = jnp.broadcast_to(shift_div(w, 128).astype(F32), (LANES, lanes)).astype(BF16)
+    low = jnp.broadcast_to((w & 127).astype(F32), (LANES, lanes)).astype(BF16)
+    tally = nt_dot(hot, high) * 128.0 + nt_dot(hot, low)
+    wide = jnp.concatenate([jnp.maximum(tally, 1.0)] * (half // LANES), axis=1)
+    left, right = totals[0] / wide, totals[1] / wide
+    square = jnp.sum(left * left + right * right, axis=1, keepdims=True)
+    norm = jnp.sqrt(square + 1e-06)
+    means_ref[:, :half] = left
+    means_ref[:, half:] = right
+    cent_ref[:, :half] = left / norm
+    cent_ref[:, half:] = right / norm
+
+
+VMEM_SPEC = pl.BlockSpec(memory_space=pltpu.VMEM)
+SMEM_SPEC = pl.BlockSpec(memory_space=pltpu.SMEM)
+
+
+def body(points, assignment, sample_index):
+    count_pts, features = points.shape
+    half = features // 2
+    sizes = tuple(lax.axis_size(a) for a in ("gx", "gy", "gz"))
+    n_gx, n_gy, n_gz = sizes
+    n_plane = n_gx * n_gz
+    devices = n_gx * n_gy * n_gz
+    capacity = 2 * count_pts // devices
+
+    def room(groups, slack, most):
+        return min(8 * ((5 * count_pts // (8 * groups) + slack + 7) // 8), 8 * (most // 8 + 1), LANES)
+
+    room_a1 = room(n_gy, count_pts // 16, n_plane * capacity)
+    room_b1 = room(n_plane, count_pts // 16, n_gy * capacity)
+    room_a2 = room(n_plane, count_pts * 5 // 64, n_gy * capacity)
+    room_b2 = room(n_gy, count_pts * 3 // 32, n_plane * capacity)
+    my_gx, my_gy, my_gz = (lax.axis_index(a) for a in ("gx", "gy", "gz"))
+    gy_id = my_gy.astype(I32).reshape(1)
+    me = ((my_gx * n_gy + my_gy) * n_gz + my_gz).astype(I32).reshape(1)
+
+    def along_gy(blocks):
+        return [blocks[0]] + [
+            lax.ppermute(blocks[s], "gy", [(i, (i + s) % n_gy) for i in range(n_gy)])
+            for s in range(1, n_gy)
+        ]
+
+    def in_plane(blocks):
+        return lax.all_to_all(blocks, ("gx", "gz"), split_axis=0, concat_axis=0, tiled=True)
+
+    def shape(*dims):
+        return jax.ShapeDtypeStruct(dims, F32)
+
+    sent = pl.pallas_call(
+        functools.partial(prepare_kernel, sizes, (room_a1, room_b1)),
+        in_specs=[SMEM_SPEC] + [VMEM_SPEC] * 3,
+        out_specs=[VMEM_SPEC] * (n_gy + 1),
+        out_shape=[shape(room_a1, half)] * n_gy + [shape(n_plane, room_b1, half)],
+        name="prepare",
+    )(gy_id, points, assignment.reshape(1, count_pts), sample_index.reshape(1, count_pts))
+    a1 = along_gy(sent[:n_gy])
+    b1 = in_plane(sent[n_gy])
+    sent = pl.pallas_call(
+        functools.partial(forward_kernel, sizes, (room_a2, room_b2)),
+        in_specs=[SMEM_SPEC] + [VMEM_SPEC] * (n_gy + 1),
+        out_specs=[VMEM_SPEC] * (n_gy + 1),
+        out_shape=[shape(n_plane, room_a2, half)] + [shape(room_b2, half)] * n_gy,
+        name="forward",
+    )(gy_id, *a1, b1)
+    b2 = along_gy(sent[1:])
+    a2 = in_plane(sent[0])
+    flag = jnp.max(a2[:, room_a2 - 1, 2 * LANES : 3 * LANES], axis=0)
+    flags = along_gy([flag] * n_gy)
+    over = functools.reduce(jnp.maximum, flags)[0] > 0.0
+
+    def finish(points, assignment, sample_index, a2, *b2):
+        steps = 4
+        block = CL_DEV // steps
+        lanes_a, lanes_b = n_plane * LANES, n_gy * LANES
+        return tuple(
+            pl.pallas_call(
+                functools.partial(finish_kernel, sizes, steps),
+                grid=(steps,),
+                in_specs=[SMEM_SPEC] + [VMEM_SPEC] * (n_gy + 1),
+                out_specs=[pl.BlockSpec((block, features), lambda i: (i, 0))] * 2,
+                out_shape=[shape(CL_DEV, features)] * 2,
+                scratch_shapes=[
+                    pltpu.VMEM((3, lanes_a, half), BF16),
+                    pltpu.VMEM((3, lanes_b, half), BF16),
+                    pltpu.VMEM((8, lanes_a), I32),
+                    pltpu.VMEM((8, lanes_b), I32),
+                ],
+                compiler_params=pltpu.CompilerParams(dimension_semantics=("arbitrary",)),
+                name="finish",
+            )(me, a2, *b2)
+        )
+
+    def again(points, assignment, sample_index, a2, *b2):
+        return full_body(points, assignment, sample_index)
+
+    return lax.cond(over, again, finish, points, assignment, sample_index, a2, *b2)
+
+
 def solution(mesh):
     return jax.shard_map(
         body,

time: 145 us -> 72 us (0.50)
  waiting for transfers between devices: 74.3 us -> 23.1 us
  Pallas kernels: 0 us -> 19.8 us
  matrix products: 17.8 us -> 0 us
  other arithmetic: 17.4 us -> 0.03 us
  local copies, waits for them, and re-layouts: 16.2 us -> 1.01 us
  starting transfers between devices: 16.7 us -> 27 us
    all_to_all x3 -> x2, waiting for transfers between devices: 74.3 us -> 7.28 us  [in_plane(): lax.all_to_all(blocks, ('gx', 'gz'), split_axis=0, concat_axis=0, tiled=T...]
    pallas_call x0 -> x3, Pallas kernels: none -> 19.8 us  [the longest x1 8.36 us: finish(): pl.pallas_call(functools.partial(finish_kernel, sizes, steps), grid=(step...]
    ppermute x0 -> x9, starting transfers between devices: none -> 18 us  [along_gy(): lax.ppermute(blocks[s], 'gy', [(i, (i + s) % n_gy) for i in range(n_gy)])]
    dot_general x3 -> x0, matrix products: 17.8 us -> none  [the longest x2 17.6 us: accumulate(): jnp.einsum('rk,rd->kd', onehot, rows_b, precision=lax.Precision.HIGHEST)]
    ppermute x0 -> x9, waiting for transfers between devices: none -> 15.9 us  [along_gy(): lax.ppermute(blocks[s], 'gy', [(i, (i + s) % n_gy) for i in range(n_gy)])]
    all_to_all x3 -> x2, starting transfers between devices: 16.7 us -> 9.01 us  [in_plane(): lax.all_to_all(blocks, ('gx', 'gz'), split_axis=0, concat_axis=0, tiled=T...]
    scatter x3 -> x0, local copies, waits for them, and re-layouts: 7.34 us -> none  [the longest x1 2.45 us: body(): source = jnp.zeros((devices * capacity,), jnp.int32).at[slot].set(point_ids)]
    gather x1 -> x0, local copies, waits for them, and re-layouts: 5.22 us -> none  [body(): rows = jnp.take(points, source, axis=0)]
  transfers between devices with their start and end apart: 3 -> 11, of which waited for: 2 -> 6; matrix products, arithmetic and copies ran while one was open for 14% -> 0% of each run, Pallas kernels for 0% -> 0%
where the time goes in v1:
time: 72 us; the launch traced here: 71.7 us
  starting transfers between devices  27 us (38%)
  waiting for transfers between devices  23.1 us (32%)
  Pallas kernels  19.8 us (28%)
  local copies, waits for them, and re-layouts  1.01 us (1%)
  between operations  0.77 us (1%)
    ppermute x9, starting transfers between devices, along_gy(): lax.ppermute(blocks[s], 'gy', [(i, (i + s) % n_gy) for i in range(n_gy)])  18 us
    ppermute x9, waiting for transfers between devices, along_gy(): lax.ppermute(blocks[s], 'gy', [(i, (i + s) % n_gy) for i in range(n_gy)])  15.9 us
    all_to_all x2, starting transfers between devices, in_plane(): lax.all_to_all(blocks, ('gx', 'gz'), split_axis=0, concat_axis=0, tiled=T...  9.01 us
    pallas_call x1, Pallas kernels, finish(): pl.pallas_call(functools.partial(finish_kernel, sizes, steps), grid=(step...  8.36 us
    all_to_all x2, waiting for transfers between devices, in_plane(): lax.all_to_all(blocks, ('gx', 'gz'), split_axis=0, concat_axis=0, tiled=T...  7.28 us
    pallas_call x1, Pallas kernels, body(): pl.pallas_call(functools.partial(forward_kernel, sizes, (room_a2, room_b2...  6.03 us
    pallas_call x1, Pallas kernels, body(): pl.pallas_call(functools.partial(prepare_kernel, sizes, (room_a1, room_b1...  5.36 us
  transfers between devices with their start and end apart: 11, of which 6 were waited for; matrix products, arithmetic and copies ran while one was open for 0% of the time, Pallas kernels for 0%

profile of v1, /device:TPU:0, one launch (start us, length us, event | category | flops | bytes accessed | tf_op | source)
XLA Modules:
  0.0 71.7 jit_solution(1530598270034612313)
XLA Ops:
  0.7 5.4 %prepare.1 = (f32[112,384]{1,0:T(8,128)}, f32[112,384]{1,0:T(8,128)}, f32[112,384]{1,0:T(8,128)}, f32[112,384]{1,0:T(8,128)}, f32[8,72,384]{2,1,0:T(8,128)}) custom-call(s32[1]{0:T(128)} %bitcast.3.my_ref, f32[512,768]{1,0:T(8,128)} %points_ref.1, s32[1,512]{1,0:T(1,128)} %bitcast.15, s32[1,512]{1,0:T(1,128)} %bitcast.16), custom_call_target="tpu_custom_call" | custom-call | tf_op jit(solution)/shard_map/prepare/pallas_call | solution.py:335
  6.0 5.2 %all-to-all-start.3 = ((f32[8,72,384]{2,1,0:T(8,128)}), f32[8,72,384]{2,1,0:T(8,128)S(1)}, u32[]{:S(2)}, u32[]{:S(2)}) async-start(f32[8,72,384]{2,1,0:T(8,128)} %get-tuple-element.99), calls=%async_computation.3 | async-start | bytes 1769472 | tf_op jit(solution)/shard_map/all_to_all | solution.py:330
  11.2 1.6 %collective-permute-start = (f32[112,384]{1,0:T(8,128)}, f32[112,384]{1,0:T(8,128)S(1)}, u32[]{:S(2)}, u32[]{:S(2)}) collective-permute-start(f32[112,384]{1,0:T(8,128)} %get-tuple-element.96), channel_id=1, source_target_pairs={{0,2},{2,4},{4,6},{6,0},{1,3},{3,5},{5,7},{7,1},{8,10},{10,12},{12... | collective-permute-start | bytes 516104 | tf_op jit(solution)/shard_map/ppermute | solution.py:325
  12.8 2.6 %collective-permute-start.1 = (f32[112,384]{1,0:T(8,128)}, f32[112,384]{1,0:T(8,128)S(1)}, u32[]{:S(2)}, u32[]{:S(2)}) collective-permute-start(f32[112,384]{1,0:T(8,128)} %get-tuple-element.97), channel_id=1, source_target_pairs={{0,4},{2,6},{4,0},{6,2},{1,5},{3,7},{5,1},{7,3},{8,12},{10,14},{12... | collective-permute-start | bytes 516104 | tf_op jit(solution)/shard_map/ppermute | solution.py:325
  15.4 1.3 %collective-permute-start.2 = (f32[112,384]{1,0:T(8,128)}, f32[112,384]{1,0:T(8,128)S(1)}, u32[]{:S(2)}, u32[]{:S(2)}) collective-permute-start(f32[112,384]{1,0:T(8,128)} %get-tuple-element.98), channel_id=1, source_target_pairs={{0,6},{2,0},{4,2},{6,4},{1,7},{3,1},{5,3},{7,5},{8,14},{10,8},{12,... | collective-permute-start | bytes 516104 | tf_op jit(solution)/shard_map/ppermute | solution.py:325
  16.7 3.9 %collective-permute-done.refs_1_ = f32[112,384]{1,0:T(8,128)S(1)} collective-permute-done((f32[112,384]{1,0:T(8,128)}, f32[112,384]{1,0:T(8,128)S(1)}, u32[]{:S(2)}, u32[]{:S(2)}) %collective-permute-start) | collective-permute-done | bytes 172064 | tf_op jit(solution)/shard_map/ppermute | solution.py:325
  20.6 6.9 %collective-permute-done.1.refs_2_ = f32[112,384]{1,0:T(8,128)S(1)} collective-permute-done((f32[112,384]{1,0:T(8,128)}, f32[112,384]{1,0:T(8,128)S(1)}, u32[]{:S(2)}, u32[]{:S(2)}) %collective-permute-start.1) | collective-permute-done | bytes 172064 | tf_op jit(solution)/shard_map/ppermute | solution.py:325
  27.6 0.6 copy-done.3
  28.2 0.1 copy-done.4
  28.3 0.3 copy-done.1
  28.6 6.0 %forward.1 = (f32[8,80,384]{2,1,0:T(8,128)}, f32[128,384]{1,0:T(8,128)S(1)}, f32[128,384]{1,0:T(8,128)}, f32[128,384]{1,0:T(8,128)}, f32[128,384]{1,0:T(8,128)}) custom-call(s32[1]{0:T(128)} %bitcast.3.my_ref, f32[112,384]{1,0:T(8,128)} %get-tuple-element.95.refs_0_, f32[112,384]{1,0:T(8,128)} %copy-done.2, f32[112,384]{1,0:T(8,128)} %copy-done.3, ...), custom_call_target="tpu_custom_call" | custom-call | tf_op jit(solution)/shard_map/forward/pallas_call | solution.py:344
  34.6 3.8 %all-to-all-start.4 = ((f32[8,80,384]{2,1,0:T(8,128)}), f32[8,80,384]{2,1,0:T(8,128)S(1)}, u32[]{:S(2)}, u32[]{:S(2)}) async-start(f32[8,80,384]{2,1,0:T(8,128)} %get-tuple-element.100), calls=%async_computation.4 | async-start | bytes 1966080 | tf_op jit(solution)/shard_map/all_to_all | solution.py:330
  38.4 4.1 %collective-permute-start.6 = (f32[128,384]{1,0:T(8,128)}, f32[128,384]{1,0:T(8,128)S(1)}, u32[]{:S(2)}, u32[]{:S(2)}) collective-permute-start(f32[128,384]{1,0:T(8,128)} %get-tuple-element.102), channel_id=1, source_target_pairs={{0,2},{2,4},{4,6},{6,0},{1,3},{3,5},{5,7},{7,1},{8,10},{10,12},{12... | collective-permute-start | bytes 589832 | tf_op jit(solution)/shard_map/ppermute | solution.py:325
  42.5 1.7 %collective-permute-start.7 = (f32[128,384]{1,0:T(8,128)}, f32[128,384]{1,0:T(8,128)S(1)}, u32[]{:S(2)}, u32[]{:S(2)}) collective-permute-start(f32[128,384]{1,0:T(8,128)} %get-tuple-element.103), channel_id=1, source_target_pairs={{0,4},{2,6},{4,0},{6,2},{1,5},{3,7},{5,1},{7,3},{8,12},{10,14},{12... | collective-permute-start | bytes 589832 | tf_op jit(solution)/shard_map/ppermute | solution.py:325
  44.2 0.8 %collective-permute-start.8 = (f32[128,384]{1,0:T(8,128)}, f32[128,384]{1,0:T(8,128)S(1)}, u32[]{:S(2)}, u32[]{:S(2)}) collective-permute-start(f32[128,384]{1,0:T(8,128)} %get-tuple-element.104), channel_id=1, source_target_pairs={{0,6},{2,0},{4,2},{6,4},{1,7},{3,1},{5,3},{7,5},{8,14},{10,8},{12,... | collective-permute-start | bytes 589832 | tf_op jit(solution)/shard_map/ppermute | solution.py:325
  45.0 7.3 %all-to-all-done.4 = f32[8,80,384]{2,1,0:T(8,128)S(1)} async-done(((f32[8,80,384]{2,1,0:T(8,128)}), f32[8,80,384]{2,1,0:T(8,128)S(1)}, u32[]{:S(2)}, u32[]{:S(2)}) %all-to-all-start.4) | async-done | bytes 983072 | tf_op jit(solution)/shard_map/all_to_all | solution.py:330
  52.3 5.3 %collective-permute-start.5 = (f32[128]{0:T(128)S(1)}, f32[128]{0:T(128)S(1)}, u32[]{:S(2)}, u32[]{:S(2)}) collective-permute-start(f32[128]{0:T(128)S(1)} %slice_reduce_fusion), channel_id=1, source_target_pairs={{0,6},{2,0},{4,2},{6,4},{1,7},{3,1},{5,3},{7,5},{8,14},{10,8},{12,... | collective-permute-start | bytes 1544 | tf_op jit(solution)/shard_map/ppermute | solution.py:325
  57.5 0.3 collective-permute-start.4
  57.9 0.3 collective-permute-start.3
  58.2 0.6 collective-permute-done.5
  58.8 3.3 %collective-permute-done.4 = f32[128]{0:T(128)S(1)} collective-permute-done((f32[128]{0:T(128)S(1)}, f32[128]{0:T(128)S(1)}, u32[]{:S(2)}, u32[]{:S(2)}) %collective-permute-start.4) | collective-permute-done | bytes 544 | tf_op jit(solution)/shard_map/ppermute | solution.py:325
  62.1 1.1 %collective-permute-done.3 = f32[128]{0:T(128)S(1)} collective-permute-done((f32[128]{0:T(128)S(1)}, f32[128]{0:T(128)S(1)}, u32[]{:S(2)}, u32[]{:S(2)}) %collective-permute-start.3) | collective-permute-done | bytes 544 | tf_op jit(solution)/shard_map/ppermute | solution.py:325
  63.3 8.4 %conditional.1 = ((f32[1024,768]{1,0:T(8,128)}, f32[1024,768]{1,0:T(8,128)})) conditional(s32[]{:T(128)} %bitcast.6, (s32[]{:T(128)}, s32[]{:T(128)}, s32[]{:T(128)}, f32[8,80,384]{2,1,0:T(8,128)S(1)}, f32[128,384]{1,0:T(8,128)S(1)}, /*index=5*/f32[128,384]{1,0:T(8,128)S(1)}, f32[128,384]{1,0:T(8,128)S(1)}, f32[128,384]{1,0:T(8,128)S(1)}) %tuple.22, ...), branch_computations={%region_1.0_spmd, %region_2.12_spmd} | conditional | flops 4857097728 | bytes 42715592 | solution.py:382
  63.4 8.4 %finish.1 = (f32[1024,768]{1,0:T(8,128)}, f32[1024,768]{1,0:T(8,128)}) custom-call(s32[1]{0:T(128)} %bitcast.my_ref, f32[8,80,384]{2,1,0:T(8,128)S(1)} %get-tuple-element.64.refs_0_, f32[128,384]{1,0:T(8,128)S(1)} %get-tuple-element.65.refs_1_, f32[128,384]{1,0:T(8,128)S(1)} %get-tuple-element.66.refs_2_, f32[128,384]{1,0:T(8,128)S(1)} %get-tuple-element.67.refs_3_, ...), custom_call_target="tpu_custom_call" | custom-call | tf_op jit(solution)/shard_map/cond/branch_0_fun/finish/pallas_call | solution.py:362
  (18 shorter events, 0.1 us)
Async XLA Ops:
  0.6 62.7 %copy-start = (f32[512,768]{1,0:T(8,128)S(1)}, f32[512,768]{1,0:T(8,128)}, u32[]{:S(2)}) copy-start(f32[512,768]{1,0:T(8,128)} %points_ref.1) | copy-start | bytes 4718596
  0.6 62.7 %copy-start.5 = (s32[512]{0:T(512)S(1)}, s32[512]{0:T(512)}, u32[]{:S(2)}) copy-start(s32[512]{0:T(512)} %param.8) | copy-start | bytes 6148
  0.7 62.7 %copy-start.6 = (s32[512]{0:T(512)S(1)}, s32[512]{0:T(512)}, u32[]{:S(2)}) copy-start(s32[512]{0:T(512)} %param.9) | copy-start | bytes 6148
  6.0 21.5 %all-to-all-start.3 = ((f32[8,72,384]{2,1,0:T(8,128)}), f32[8,72,384]{2,1,0:T(8,128)S(1)}, u32[]{:S(2)}, u32[]{:S(2)}) async-start(f32[8,72,384]{2,1,0:T(8,128)} %get-tuple-element.99), calls=%async_computation.3 | async-start | bytes 1769472 | tf_op jit(solution)/shard_map/all_to_all | solution.py:330
  11.2 9.4 %collective-permute-start = (f32[112,384]{1,0:T(8,128)}, f32[112,384]{1,0:T(8,128)S(1)}, u32[]{:S(2)}, u32[]{:S(2)}) collective-permute-start(f32[112,384]{1,0:T(8,128)} %get-tuple-element.96), channel_id=1, source_target_pairs={{0,2},{2,4},{4,6},{6,0},{1,3},{3,5},{5,7},{7,1},{8,10},{10,12},{12... | collective-permute-start | bytes 516104 | tf_op jit(solution)/shard_map/ppermute | solution.py:325
  12.8 14.7 %collective-permute-start.1 = (f32[112,384]{1,0:T(8,128)}, f32[112,384]{1,0:T(8,128)S(1)}, u32[]{:S(2)}, u32[]{:S(2)}) collective-permute-start(f32[112,384]{1,0:T(8,128)} %get-tuple-element.97), channel_id=1, source_target_pairs={{0,4},{2,6},{4,0},{6,2},{1,5},{3,7},{5,1},{7,3},{8,12},{10,14},{12... | collective-permute-start | bytes 516104 | tf_op jit(solution)/shard_map/ppermute | solution.py:325
  15.4 12.1 %collective-permute-start.2 = (f32[112,384]{1,0:T(8,128)}, f32[112,384]{1,0:T(8,128)S(1)}, u32[]{:S(2)}, u32[]{:S(2)}) collective-permute-start(f32[112,384]{1,0:T(8,128)} %get-tuple-element.98), channel_id=1, source_target_pairs={{0,6},{2,0},{4,2},{6,4},{1,7},{3,1},{5,3},{7,5},{8,14},{10,8},{12,... | collective-permute-start | bytes 516104 | tf_op jit(solution)/shard_map/ppermute | solution.py:325
  20.6 7.0 %copy-start.2 = (f32[112,384]{1,0:T(8,128)}, f32[112,384]{1,0:T(8,128)S(1)}, u32[]{:S(2)}) copy-start(f32[112,384]{1,0:T(8,128)S(1)} %collective-permute-done.refs_1_) | copy-start | bytes 516100
  27.5 0.7 copy-start.3
  27.5 0.7 %copy-start.4 = (f32[112,384]{1,0:T(8,128)}, f32[112,384]{1,0:T(8,128)S(1)}, u32[]{:S(2)}) copy-start(f32[112,384]{1,0:T(8,128)S(1)} %collective-permute-done.2.refs_3_) | copy-start | bytes 516100
  27.6 1.0 %copy-start.1 = (f32[8,72,384]{2,1,0:T(8,128)}, f32[8,72,384]{2,1,0:T(8,128)S(1)}, u32[]{:S(2)}) copy-start(f32[8,72,384]{2,1,0:T(8,128)S(1)} %all-to-all-done.3.refs_4_) | copy-start | bytes 2654212
  34.6 17.6 %all-to-all-start.4 = ((f32[8,80,384]{2,1,0:T(8,128)}), f32[8,80,384]{2,1,0:T(8,128)S(1)}, u32[]{:S(2)}, u32[]{:S(2)}) async-start(f32[8,80,384]{2,1,0:T(8,128)} %get-tuple-element.100), calls=%async_computation.4 | async-start | bytes 1966080 | tf_op jit(solution)/shard_map/all_to_all | solution.py:330
  38.4 19.5 %collective-permute-start.6 = (f32[128,384]{1,0:T(8,128)}, f32[128,384]{1,0:T(8,128)S(1)}, u32[]{:S(2)}, u32[]{:S(2)}) collective-permute-start(f32[128,384]{1,0:T(8,128)} %get-tuple-element.102), channel_id=1, source_target_pairs={{0,2},{2,4},{4,6},{6,0},{1,3},{3,5},{5,7},{7,1},{8,10},{10,12},{12... | collective-permute-start | bytes 589832 | tf_op jit(solution)/shard_map/ppermute | solution.py:325
  42.5 15.7 %collective-permute-start.7 = (f32[128,384]{1,0:T(8,128)}, f32[128,384]{1,0:T(8,128)S(1)}, u32[]{:S(2)}, u32[]{:S(2)}) collective-permute-start(f32[128,384]{1,0:T(8,128)} %get-tuple-element.103), channel_id=1, source_target_pairs={{0,4},{2,6},{4,0},{6,2},{1,5},{3,7},{5,1},{7,3},{8,12},{10,14},{12... | collective-permute-start | bytes 589832 | tf_op jit(solution)/shard_map/ppermute | solution.py:325
  44.2 14.0 %collective-permute-start.8 = (f32[128,384]{1,0:T(8,128)}, f32[128,384]{1,0:T(8,128)S(1)}, u32[]{:S(2)}, u32[]{:S(2)}) collective-permute-start(f32[128,384]{1,0:T(8,128)} %get-tuple-element.104), channel_id=1, source_target_pairs={{0,6},{2,0},{4,2},{6,4},{1,7},{3,1},{5,3},{7,5},{8,14},{10,8},{12,... | collective-permute-start | bytes 589832 | tf_op jit(solution)/shard_map/ppermute | solution.py:325
  52.3 6.6 %collective-permute-start.5 = (f32[128]{0:T(128)S(1)}, f32[128]{0:T(128)S(1)}, u32[]{:S(2)}, u32[]{:S(2)}) collective-permute-start(f32[128]{0:T(128)S(1)} %slice_reduce_fusion), channel_id=1, source_target_pairs={{0,6},{2,0},{4,2},{6,4},{1,7},{3,1},{5,3},{7,5},{8,14},{10,8},{12,... | collective-permute-start | bytes 1544 | tf_op jit(solution)/shard_map/ppermute | solution.py:325
  57.5 4.6 %collective-permute-start.4 = (f32[128]{0:T(128)S(1)}, f32[128]{0:T(128)S(1)}, u32[]{:S(2)}, u32[]{:S(2)}) collective-permute-start(f32[128]{0:T(128)S(1)} %slice_reduce_fusion), channel_id=1, source_target_pairs={{0,4},{2,6},{4,0},{6,2},{1,5},{3,7},{5,1},{7,3},{8,12},{10,14},{12... | collective-permute-start | bytes 1544 | tf_op jit(solution)/shard_map/ppermute | solution.py:325
  57.9 5.4 %collective-permute-start.3 = (f32[128]{0:T(128)S(1)}, f32[128]{0:T(128)S(1)}, u32[]{:S(2)}, u32[]{:S(2)}) collective-permute-start(f32[128]{0:T(128)S(1)} %slice_reduce_fusion), channel_id=1, source_target_pairs={{0,2},{2,4},{4,6},{6,0},{1,3},{3,5},{5,7},{7,1},{8,10},{10,12},{12... | collective-permute-start | bytes 1544 | tf_op jit(solution)/shard_map/ppermute | solution.py:325

commit v2 on v0

--- a/solution.py
+++ b/solution.py
@@ -1,14 +1,23 @@
+import functools
 import math
 
 import jax
 import jax.numpy as jnp
 from jax import lax
+from jax.experimental import pallas as pl
+from jax.experimental.pallas import tpu as pltpu
 from jax.sharding import PartitionSpec as P
 
+
 CL_DEV = 1024
-
-
-def body(points, assignment, sample_index):
+LANES = 128
+F32 = jnp.float32
+BF16 = jnp.bfloat16
+PARTS = 3
+I32 = jnp.int32
+
+
+def full_body(points, assignment, sample_index):
     count_pts, features = points.shape
     size_gx = lax.axis_size("gx")
     rest = lax.axis_size("gy") * lax.axis_size("gz")
@@ -80,6 +89,378 @@
     return (means, centroids)
 
 
+def shift_div(x, n):
+    return lax.shift_right_logical(x, jnp.int32(n.bit_length() - 1))
+
+
+def iota(shape, dim):
+    return lax.broadcasted_iota(I32, shape, dim)
+
+
+def as_bf16(mask):
+    return jnp.where(mask, 1.0, 0.0).astype(BF16)
+
+
+def nt_dot(a, b):
+    return lax.dot_general(a, b, (((1,), (1,)), ((), ())), preferred_element_type=F32)
+
+
+def nn_dot(a, b):
+    return jnp.dot(a, b, preferred_element_type=F32)
+
+
+def split(x):
+    parts = []
+    for _ in range(PARTS):
+        parts.append(x.astype(BF16))
+        x = x - parts[-1].astype(F32)
+    return parts
+
+
+def place(hot):
+    groups, lanes = hot.shape
+    upper = as_bf16(iota((LANES, LANES), 0) < iota((LANES, LANES), 1))
+    run = jnp.zeros((groups, 1), F32)
+    places = []
+    for start in range(0, lanes, LANES):
+        width = min(LANES, lanes - start)
+        h = hot[:, start : start + width]
+        before = nn_dot(h.astype(BF16), upper[:width, :width]) + run
+        places.append(jnp.sum(before * h, axis=0, keepdims=True))
+        run = run + jnp.sum(h, axis=1, keepdims=True)
+    return jnp.concatenate(places, axis=1), jnp.max(run)
+
+
+def pack(parts, ids, weight, group, groups, room, write):
+    lanes = ids.shape[1]
+    valid = weight > 0.0
+    hot = jnp.where((iota((groups, lanes), 0) == group) & valid, 1.0, 0.0)
+    pos, most = place(hot)
+    pos = pos.astype(I32)
+    keep = valid & (pos < room - 1)
+    slot = jnp.where(keep, group * room + pos, -1)
+    pick = as_bf16(iota((groups * room, lanes), 0) == slot)
+    out = functools.reduce(jnp.add, [nn_dot(pick, part) for part in parts])
+    w = weight.astype(I32)
+    pieces = [
+        shift_div(ids, 16384),
+        shift_div(ids, 128) & 127,
+        ids & 127,
+        shift_div(w, 128),
+        w & 127,
+    ]
+    row = iota((8, lanes), 0)
+    stack = jnp.zeros((8, lanes), F32)
+    for k, piece in enumerate(pieces):
+        stack = jnp.where(row == k, piece.astype(F32), stack)
+    tags = nt_dot(stack.astype(BF16), pick)
+    tag_ids = tags[0:1] * 16384.0 + tags[1:2] * 128.0 + tags[2:3]
+    tag_w = tags[3:4] * 128.0 + tags[4:5]
+    for g in range(groups):
+        span = slice(g * room, (g + 1) * room)
+        write(g, out[span], tag_ids[:, span], tag_w[:, span])
+    return most
+
+
+def flag_row(flag):
+    return jnp.where(iota((1, LANES), 1) == LANES - 1, jnp.full((1, LANES), 1.0, F32) * flag, 0.0)
+
+
+def padded(row):
+    width = row.shape[1]
+    if width == LANES:
+        return row
+    return jnp.concatenate([row, jnp.zeros((1, LANES - width), F32)], axis=1)
+
+
+def write_block(ref, at, room, rows, tag_ids, tag_w):
+    ref[at + (slice(0, room), slice(None))] = rows
+    last = slice(room - 1, room)
+    ref[at + (last, slice(0, LANES))] = padded(tag_ids)
+    ref[at + (last, slice(LANES, 2 * LANES))] = padded(tag_w)
+
+
+def write_news(ref, at, room, flag, counts):
+    last = slice(room - 1, room)
+    lane = iota((1, LANES), 1)
+    ids = ref[at + (last, slice(0, LANES))]
+    ref[at + (last, slice(0, LANES))] = jnp.where(lane == LANES - 1, flag_row(flag), ids)
+    ref[at + (last, slice(2 * LANES, 3 * LANES))] = counts
+
+
+def above(most, room):
+    return jnp.where(most > room - 1, 1.0, 0.0)
+
+
+def gy_shift(gy, me, sizes):
+    _, n_gy, n_gz = sizes
+    return (gy - (shift_div(me, n_gz) & (n_gy - 1)) + n_gy) & (n_gy - 1)
+
+
+def split_owner(ids, sizes):
+    _, n_gy, n_gz = sizes
+    owner = shift_div(ids, CL_DEV)
+    gz = owner & (n_gz - 1)
+    gy = shift_div(owner, n_gz) & (n_gy - 1)
+    gx = shift_div(owner, n_gz * n_gy)
+    return gy, gx * n_gz + gz
+
+
+def prepare_a_kernel(sizes, room, my_ref, x_ref, assign_ref, index_ref, *outs):
+    _, n_gy, _ = sizes
+    a_refs, weight_ref, wide_ref = outs[:n_gy], outs[n_gy], outs[n_gy + 1]
+    count_pts, half = x_ref.shape
+    ids = assign_ref[...]
+    hot = as_bf16(iota((count_pts, count_pts), 0) == index_ref[...])
+    weight = nt_dot(jnp.ones((8, count_pts), BF16), hot)[0:1]
+    weight_ref[...] = weight
+    weight_col = nn_dot(hot, jnp.ones((count_pts, LANES), BF16))
+    wide_ref[...] = weight_col
+    wide = jnp.concatenate([weight_col] * (half // LANES), axis=1)
+    gy, _ = split_owner(ids, sizes)
+    shift = gy_shift(gy, my_ref[0], sizes)
+    most = pack(
+        split(x_ref[...] * wide), ids, weight, shift, n_gy, room,
+        lambda g, *v: write_block(a_refs[g], (), room, *v),
+    )
+    counts = demand(ids, weight)
+    for g in range(n_gy):
+        write_news(a_refs[g], (), room, above(most, room), counts)
+
+
+def prepare_b_kernel(sizes, room, x_ref, assign_ref, weight_ref, wide_ref, b_ref):
+    n_gx, _, n_gz = sizes
+    half = x_ref.shape[1]
+    ids, weight = assign_ref[...], weight_ref[...]
+    wide = jnp.concatenate([wide_ref[...]] * (half // LANES), axis=1)
+    _, plane = split_owner(ids, sizes)
+    most = pack(
+        split(x_ref[...] * wide), ids, weight, plane, n_gx * n_gz, room,
+        lambda g, *v: write_block(b_ref, (g,), room, *v),
+    )
+    counts = demand(ids, weight)
+    for g in range(n_gx * n_gz):
+        write_news(b_ref, (g,), room, above(most, room), counts)
+
+
+def demand(ids, weight):
+    owner = shift_div(ids, CL_DEV)
+    hot = as_bf16(iota((LANES, ids.shape[1]), 0) == owner)
+    return nt_dot(jnp.where(jnp.broadcast_to(weight, (8, ids.shape[1])) > 0.0, 1.0, 0.0).astype(BF16), hot)[0:1]
+
+
+def gathered(blocks):
+    rows, ids, weight = [], [], []
+    first, counts = jnp.zeros((1, LANES), F32), jnp.zeros((1, LANES), F32)
+    for block in blocks:
+        room = block.shape[0]
+        rows.append(block)
+        last = block[room - 1 : room]
+        ids.append(last[:, :room])
+        weight.append(last[:, LANES : LANES + room])
+        first = jnp.maximum(first, last[:, :LANES])
+        counts = counts + last[:, 2 * LANES : 3 * LANES]
+    flag = jnp.max(jnp.where(iota((1, LANES), 1) == LANES - 1, first, 0.0))
+    return (
+        jnp.concatenate(rows, axis=0),
+        jnp.concatenate(ids, axis=1).astype(I32),
+        jnp.concatenate(weight, axis=1),
+        flag,
+        counts,
+    )
+
+
+def forward_b_kernel(sizes, room, my_ref, b_in, *b_out):
+    n_gx, n_gy, n_gz = sizes
+    rows, ids, weight, flag, counts = gathered([b_in[g] for g in range(n_gx * n_gz)])
+    gy, _ = split_owner(ids, sizes)
+    pack(
+        split(rows), ids, weight, gy_shift(gy, my_ref[0], sizes), n_gy, room,
+        lambda g, *v: write_block(b_out[g], (), room, *v),
+    )
+    flag = jnp.maximum(flag, above(jnp.max(counts), room))
+    for g in range(n_gy):
+        write_news(b_out[g], (), room, flag, counts)
+
+
+def forward_a_kernel(sizes, room, *refs):
+    n_gx, n_gy, n_gz = sizes
+    a_in, a_out = refs[:n_gy], refs[n_gy]
+    rows, ids, weight, flag, counts = gathered([r[...] for r in a_in])
+    _, plane = split_owner(ids, sizes)
+    pack(
+        split(rows), ids, weight, plane, n_gx * n_gz, room,
+        lambda g, *v: write_block(a_out, (g,), room, *v),
+    )
+    flag = jnp.maximum(flag, above(jnp.max(counts), room))
+    for g in range(n_gx * n_gz):
+        write_news(a_out, (g,), room, flag, counts)
+
+
+def add_b_kernel(sizes, block, my_ref, *refs):
+    _, n_gy, _ = sizes
+    b_in, sum_ref, tally_ref, flag_ref = refs[:n_gy], refs[n_gy], refs[n_gy + 1], refs[n_gy + 2]
+    rows, ids, weight, flag, _ = gathered([r[...] for r in b_in])
+    flag_ref[...] = jnp.full((1, LANES), 1.0, F32) * flag
+    parts = split(rows)
+    w = weight.astype(I32)
+    target = jnp.where(w > 0, ids - my_ref[0] * CL_DEV, -1)
+    lanes = target.shape[1]
+    high = jnp.broadcast_to(shift_div(w, 128).astype(F32), (LANES, lanes)).astype(BF16)
+    low = jnp.broadcast_to((w & 127).astype(F32), (LANES, lanes)).astype(BF16)
+    for first in range(0, CL_DEV, block):
+        hot = as_bf16(iota((block, lanes), 0) + first == target)
+        sum_ref[first : first + block] = functools.reduce(jnp.add, [nn_dot(hot, p) for p in parts])
+        tally_ref[first : first + block] = nt_dot(hot, high) * 128.0 + nt_dot(hot, low)
+
+
+def finish_kernel(
+    sizes, my_ref, a_in, sum_ref, tally_ref, flag_b_ref, means_ref, cent_ref, flag_ref, x_ref, t_ref
+):
+    n_gx, _, n_gz = sizes
+    block = means_ref.shape[0]
+    half = means_ref.shape[1] // 2
+    step = pl.program_id(0)
+
+    @pl.when(step == 0)
+    def _():
+        rows, ids, weight, flag, _ = gathered([a_in[g] for g in range(n_gx * n_gz)])
+        flag_ref[0, 0] = jnp.maximum(flag, jnp.max(flag_b_ref[...]))
+        for k, part in enumerate(split(rows)):
+            x_ref[k] = part
+        t_ref[0:1, :] = jnp.where(weight > 0.0, ids - my_ref[0] * CL_DEV, -1)
+
+    first = pl.multiple_of(step * block, block)
+    lanes = t_ref.shape[1]
+    hot = as_bf16(iota((block, lanes), 0) + first == t_ref[0:1, :])
+    left = functools.reduce(jnp.add, [nn_dot(hot, x_ref[k]) for k in range(PARTS)])
+    right = sum_ref[pl.ds(first, block)]
+    share = 1.0 / jnp.maximum(tally_ref[pl.ds(first, block)], 1.0)
+    wide = jnp.concatenate([share] * (half // LANES), axis=1)
+    left, right = left * wide, right * wide
+    square = jnp.sum(left * left + right * right, axis=1, keepdims=True)
+    scale = 1.0 / jnp.sqrt(square + 1e-06)
+    means_ref[:, :half] = left
+    means_ref[:, half:] = right
+    cent_ref[:, :half] = left * scale
+    cent_ref[:, half:] = right * scale
+
+
+VMEM_SPEC = pl.BlockSpec(memory_space=pltpu.VMEM)
+SMEM_SPEC = pl.BlockSpec(memory_space=pltpu.SMEM)
+
+
+def body(points, assignment, sample_index):
+    count_pts, features = points.shape
+    half = features // 2
+    sizes = tuple(lax.axis_size(a) for a in ("gx", "gy", "gz"))
+    n_gx, n_gy, n_gz = sizes
+    n_plane = n_gx * n_gz
+    devices = n_gx * n_gy * n_gz
+    capacity = 2 * count_pts // devices
+
+    def room(groups, slack, most):
+        return min(8 * ((5 * count_pts // (8 * groups) + slack + 7) // 8), 8 * (most // 8 + 1), LANES)
+
+    room_a1 = room(n_gy, count_pts // 16, n_plane * capacity)
+    room_b1 = room(n_plane, count_pts // 16, n_gy * capacity)
+    room_a2 = room(n_plane, count_pts * 5 // 64, n_gy * capacity)
+    room_b2 = room(n_gy, count_pts * 3 // 32, n_plane * capacity)
+    my_gx, my_gy, my_gz = (lax.axis_index(a) for a in ("gx", "gy", "gz"))
+    me = ((my_gx * n_gy + my_gy) * n_gz + my_gz).astype(I32).reshape(1)
+
+    def along_gy(blocks):
+        out = [blocks[0]]
+        for s in range(1, n_gy):
+            out.append(lax.ppermute(blocks[s], "gy", [(i, (i + s) % n_gy) for i in range(n_gy)]))
+        return out
+
+    def in_plane(blocks):
+        return lax.all_to_all(blocks, ("gx", "gz"), split_axis=0, concat_axis=0, tiled=True)
+
+    def cost(us):
+        return pl.CostEstimate(flops=us * 7_000_000, bytes_accessed=1 << 20, transcendentals=0)
+
+    def vmem(mib, **others):
+        return pltpu.CompilerParams(vmem_limit_bytes=mib << 20, **others)
+
+    def shape(*dims):
+        return jax.ShapeDtypeStruct(dims, F32)
+
+    assign = assignment.reshape(1, count_pts)
+    sent = pl.pallas_call(
+        functools.partial(prepare_a_kernel, sizes, room_a1),
+        grid=(1,),
+        in_specs=[SMEM_SPEC, pl.BlockSpec((count_pts, half), lambda i: (0, 0))] + [VMEM_SPEC] * 2,
+        out_specs=[VMEM_SPEC] * (n_gy + 2),
+        out_shape=[shape(room_a1, half)] * n_gy + [shape(1, count_pts), shape(count_pts, LANES)],
+        compiler_params=vmem(12),
+        cost_estimate=cost(3),
+        name="prepare_a",
+    )(me, points, assign, sample_index.reshape(1, count_pts))
+    a1 = along_gy(sent[:n_gy])
+    sent_b = pl.pallas_call(
+        functools.partial(prepare_b_kernel, sizes, room_b1),
+        grid=(1,),
+        in_specs=[pl.BlockSpec((count_pts, half), lambda i: (0, 1))] + [VMEM_SPEC] * 3,
+        out_specs=VMEM_SPEC,
+        out_shape=shape(n_plane, room_b1, half),
+        compiler_params=vmem(12),
+        cost_estimate=cost(3),
+        name="prepare_b",
+    )(points, assign, sent[n_gy], sent[n_gy + 1])
+    b1 = in_plane(sent_b)
+    sent_a = pl.pallas_call(
+        functools.partial(forward_a_kernel, sizes, room_a2),
+        in_specs=[VMEM_SPEC] * n_gy,
+        out_specs=VMEM_SPEC,
+        out_shape=shape(n_plane, room_a2, half),
+        compiler_params=vmem(8),
+        cost_estimate=cost(3),
+        name="forward_a",
+    )(*a1)
+    a2 = in_plane(sent_a)
+    sent_b = pl.pallas_call(
+        functools.partial(forward_b_kernel, sizes, room_b2),
+        in_specs=[SMEM_SPEC, VMEM_SPEC],
+        out_specs=[VMEM_SPEC] * n_gy,
+        out_shape=[shape(room_b2, half)] * n_gy,
+        compiler_params=vmem(8),
+        cost_estimate=cost(3),
+        name="forward_b",
+    )(me, b1)
+    b2 = along_gy(sent_b)
+    block = CL_DEV // 4
+    sum_b, tally, flag_b = pl.pallas_call(
+        functools.partial(add_b_kernel, sizes, block),
+        in_specs=[SMEM_SPEC] + [VMEM_SPEC] * n_gy,
+        out_specs=[VMEM_SPEC] * 3,
+        out_shape=[shape(CL_DEV, half), shape(CL_DEV, LANES), shape(1, LANES)],
+        compiler_params=vmem(8),
+        cost_estimate=cost(3),
+        name="add_b",
+    )(me, *b2)
+    steps = 4
+    block = CL_DEV // steps
+    lanes_a = n_plane * room_a2
+    means, centroids, over = pl.pallas_call(
+        functools.partial(finish_kernel, sizes),
+        grid=(steps,),
+        in_specs=[SMEM_SPEC] + [VMEM_SPEC] * 4,
+        out_specs=[pl.BlockSpec((block, features), lambda i: (i, 0))] * 2 + [SMEM_SPEC],
+        out_shape=[shape(CL_DEV, features)] * 2 + [shape(1, 1)],
+        scratch_shapes=[pltpu.VMEM((PARTS, lanes_a, half), BF16), pltpu.VMEM((8, lanes_a), I32)],
+        compiler_params=vmem(16, dimension_semantics=("arbitrary",)),
+        cost_estimate=cost(6),
+        name="finish",
+    )(me, a2, sum_b, tally, flag_b)
+
+    def again(carry):
+        return (jnp.float32(0.0),) + full_body(points, assignment, sample_index)
+
+    return lax.while_loop(lambda carry: carry[0] > 0.0, again, (over[0, 0], means, centroids))[1:]
+
+
 def solution(mesh):
     return jax.shard_map(
         body,

time: 145 us -> 66.7 us (0.46)
  the two profiles are of different devices: /device:TPU:0 before, /device:TPU:11 now
where the time goes in v2:
time: 66.7 us; the launch traced here: 66.4 us
  waiting for transfers between devices  31 us (46%)
  Pallas kernels  18.1 us (27%)
  starting transfers between devices  15.6 us (23%)
  between operations  0.86 us (1%)
  loops' own time  0.8 us (1%)
    ppermute x6, waiting for transfers between devices, along_gy(): lax.ppermute(blocks[s], 'gy', [(i, (i + s) % n_gy) for i in range(n_gy)])  31 us
    all_to_all x2, starting transfers between devices, in_plane(): lax.all_to_all(blocks, ('gx', 'gz'), split_axis=0, concat_axis=0, tiled=T...  8.97 us
    ppermute x6, starting transfers between devices, along_gy(): lax.ppermute(blocks[s], 'gy', [(i, (i + s) % n_gy) for i in range(n_gy)])  6.64 us
    pallas_call x1, Pallas kernels, body(): pl.pallas_call(functools.partial(finish_kernel, sizes), grid=(steps,), in...  5.22 us
    pallas_call x1, Pallas kernels, body(): pl.pallas_call(functools.partial(prepare_b_kernel, sizes, room_b1), grid=...  3.52 us
    pallas_call x1, Pallas kernels, body(): pl.pallas_call(functools.partial(prepare_a_kernel, sizes, room_a1), grid=...  2.8 us
    pallas_call x1, Pallas kernels, body(): pl.pallas_call(functools.partial(forward_a_kernel, sizes, room_a2), in_sp...  2.57 us
    pallas_call x1, Pallas kernels, body(): pl.pallas_call(functools.partial(add_b_kernel, sizes, block), in_specs=[S...  2.37 us
  transfers between devices with their start and end apart: 8, of which 6 were waited for; matrix products, arithmetic and copies ran while one was open for 0% of the time, Pallas kernels for 10%

profile of v2, /device:TPU:11, one launch (start us, length us, event | category | flops | bytes accessed | tf_op | source)
XLA Modules:
  0.0 66.4 jit_solution(17433934375233618477)
XLA Ops:
  0.6 2.8 %prepare_a.1 = (f32[112,384]{1,0:T(8,128)S(1)}, f32[112,384]{1,0:T(8,128)S(1)}, f32[112,384]{1,0:T(8,128)S(1)}, f32[112,384]{1,0:T(8,128)S(1)}, f32[1,512]{1,0:T(1,128)S(1)}, /*index=5*/f32[512,128]{1,0:T(8,128)S(1)}) custom-call(s32[1]{0:T(128)} %bitcast.7.my_ref, f32[512,768]{1,0:T(8,128)} %x_ref.3, s32[1,512]{1,0:T(1,128)} %bitcast.18, s32[1,512]{1,0:T(1,128)} %bitcast.22), custom_call_target="tpu_custom_call" | custom-call | flops 21000000 | bytes 1048576 | tf_op jit(solution)/shard_map/prepare_a/pallas_call | solution.py:391
  3.4 3.5 %prepare_b.1 = f32[8,72,384]{2,1,0:T(8,128)} custom-call(f32[512,768]{1,0:T(8,128)} %x_ref.3, s32[1,512]{1,0:T(1,128)} %bitcast.19, f32[1,512]{1,0:T(1,128)S(1)} %get-tuple-element.95.weight_ref, f32[512,128]{1,0:T(8,128)S(1)} %get-tuple-element.96.wide_ref), custom_call_target="tpu_custom_call" | custom-call | flops 21000000 | bytes 1048576 | tf_op jit(solution)/shard_map/prepare_b/pallas_call | solution.py:402
  7.0 4.5 %all-to-all-start.4 = ((f32[8,72,384]{2,1,0:T(8,128)}), f32[8,72,384]{2,1,0:T(8,128)S(1)}, u32[]{:S(2)}, u32[]{:S(2)}) async-start(f32[8,72,384]{2,1,0:T(8,128)} %prepare_b.1), calls=%async_computation.4 | async-start | bytes 1769472 | tf_op jit(solution)/shard_map/all_to_all | solution.py:379
  11.5 1.3 %collective-permute-start = (f32[112,384]{1,0:T(8,128)S(1)}, f32[112,384]{1,0:T(8,128)S(1)}, u32[]{:S(2)}, u32[]{:S(2)}) collective-permute-start(f32[112,384]{1,0:T(8,128)S(1)} %get-tuple-element.92), channel_id=1, source_target_pairs={{0,2},{2,4},{4,6},{6,0},{1,3},{3,5},{5,7},{7,1},{8,10},{10,12},{12... | collective-permute-start | bytes 516104 | tf_op jit(solution)/shard_map/ppermute | solution.py:375
  12.8 1.0 %collective-permute-start.1 = (f32[112,384]{1,0:T(8,128)S(1)}, f32[112,384]{1,0:T(8,128)S(1)}, u32[]{:S(2)}, u32[]{:S(2)}) collective-permute-start(f32[112,384]{1,0:T(8,128)S(1)} %get-tuple-element.93), channel_id=1, source_target_pairs={{0,4},{2,6},{4,0},{6,2},{1,5},{3,7},{5,1},{7,3},{8,12},{10,14},{12... | collective-permute-start | bytes 516104 | tf_op jit(solution)/shard_map/ppermute | solution.py:375
  13.8 1.5 %collective-permute-start.2 = (f32[112,384]{1,0:T(8,128)S(1)}, f32[112,384]{1,0:T(8,128)S(1)}, u32[]{:S(2)}, u32[]{:S(2)}) collective-permute-start(f32[112,384]{1,0:T(8,128)S(1)} %get-tuple-element.94), channel_id=1, source_target_pairs={{0,6},{2,0},{4,2},{6,4},{1,7},{3,1},{5,3},{7,5},{8,14},{10,8},{12,... | collective-permute-start | bytes 516104 | tf_op jit(solution)/shard_map/ppermute | solution.py:375
  15.3 1.8 %collective-permute-done.refs_1_ = f32[112,384]{1,0:T(8,128)S(1)} collective-permute-done((f32[112,384]{1,0:T(8,128)S(1)}, f32[112,384]{1,0:T(8,128)S(1)}, u32[]{:S(2)}, u32[]{:S(2)}) %collective-permute-start) | collective-permute-done | bytes 172064 | tf_op jit(solution)/shard_map/ppermute | solution.py:375
  17.0 10.2 %collective-permute-done.1.refs_2_ = f32[112,384]{1,0:T(8,128)S(1)} collective-permute-done((f32[112,384]{1,0:T(8,128)S(1)}, f32[112,384]{1,0:T(8,128)S(1)}, u32[]{:S(2)}, u32[]{:S(2)}) %collective-permute-start.1) | collective-permute-done | bytes 172064 | tf_op jit(solution)/shard_map/ppermute | solution.py:375
  27.2 2.5 %collective-permute-done.2.refs_3_ = f32[112,384]{1,0:T(8,128)S(1)} collective-permute-done((f32[112,384]{1,0:T(8,128)S(1)}, f32[112,384]{1,0:T(8,128)S(1)}, u32[]{:S(2)}, u32[]{:S(2)}) %collective-permute-start.2) | collective-permute-done | bytes 172064 | tf_op jit(solution)/shard_map/ppermute | solution.py:375
  29.7 2.6 %forward_a.1 = f32[8,80,384]{2,1,0:T(8,128)} custom-call(f32[112,384]{1,0:T(8,128)S(1)} %get-tuple-element.91.refs_0_, f32[112,384]{1,0:T(8,128)S(1)} %collective-permute-done.refs_1_, f32[112,384]{1,0:T(8,128)S(1)} %collective-permute-done.1.refs_2_, f32[112,384]{1,0:T(8,128)S(1)} %collective-permute-done.2.refs_3_), custom_call_target="tpu_custom_call" | custom-call | flops 21000000 | bytes 1048576 | tf_op jit(solution)/shard_map/forward_a/pallas_call | solution.py:413
  32.3 0.0 all-to-all-done.4.b_in
  32.3 4.4 %all-to-all-start.3 = ((f32[8,80,384]{2,1,0:T(8,128)}), f32[8,80,384]{2,1,0:T(8,128)S(1)}, u32[]{:S(2)}, u32[]{:S(2)}) async-start(f32[8,80,384]{2,1,0:T(8,128)} %forward_a.1), calls=%async_computation.3 | async-start | bytes 1966080 | tf_op jit(solution)/shard_map/all_to_all | solution.py:379
  36.7 1.6 %forward_b.1 = (f32[128,384]{1,0:T(8,128)S(1)}, f32[128,384]{1,0:T(8,128)S(1)}, f32[128,384]{1,0:T(8,128)S(1)}, f32[128,384]{1,0:T(8,128)S(1)}) custom-call(s32[1]{0:T(128)} %bitcast.7.my_ref, f32[8,72,384]{2,1,0:T(8,128)S(1)} %all-to-all-done.4.b_in), custom_call_target="tpu_custom_call" | custom-call | flops 21000000 | bytes 1048576 | tf_op jit(solution)/shard_map/forward_b/pallas_call | solution.py:423
  38.3 0.1 collective-permute-start.3
  38.4 1.4 %collective-permute-start.4 = (f32[128,384]{1,0:T(8,128)S(1)}, f32[128,384]{1,0:T(8,128)S(1)}, u32[]{:S(2)}, u32[]{:S(2)}) collective-permute-start(f32[128,384]{1,0:T(8,128)S(1)} %get-tuple-element.99), channel_id=1, source_target_pairs={{0,4},{2,6},{4,0},{6,2},{1,5},{3,7},{5,1},{7,3},{8,12},{10,14},{12... | collective-permute-start | bytes 589832 | tf_op jit(solution)/shard_map/ppermute | solution.py:375
  39.8 1.4 %collective-permute-start.5 = (f32[128,384]{1,0:T(8,128)S(1)}, f32[128,384]{1,0:T(8,128)S(1)}, u32[]{:S(2)}, u32[]{:S(2)}) collective-permute-start(f32[128,384]{1,0:T(8,128)S(1)} %get-tuple-element.100), channel_id=1, source_target_pairs={{0,6},{2,0},{4,2},{6,4},{1,7},{3,1},{5,3},{7,5},{8,14},{10,8},{12,... | collective-permute-start | bytes 589832 | tf_op jit(solution)/shard_map/ppermute | solution.py:375
  41.2 3.2 %collective-permute-done.3.refs_1_ = f32[128,384]{1,0:T(8,128)S(1)} collective-permute-done((f32[128,384]{1,0:T(8,128)S(1)}, f32[128,384]{1,0:T(8,128)S(1)}, u32[]{:S(2)}, u32[]{:S(2)}) %collective-permute-start.3) | collective-permute-done | bytes 196640 | tf_op jit(solution)/shard_map/ppermute | solution.py:375
  44.5 10.7 %collective-permute-done.4.refs_2_ = f32[128,384]{1,0:T(8,128)S(1)} collective-permute-done((f32[128,384]{1,0:T(8,128)S(1)}, f32[128,384]{1,0:T(8,128)S(1)}, u32[]{:S(2)}, u32[]{:S(2)}) %collective-permute-start.4) | collective-permute-done | bytes 196640 | tf_op jit(solution)/shard_map/ppermute | solution.py:375
  55.2 2.6 %collective-permute-done.5.refs_3_ = f32[128,384]{1,0:T(8,128)S(1)} collective-permute-done((f32[128,384]{1,0:T(8,128)S(1)}, f32[128,384]{1,0:T(8,128)S(1)}, u32[]{:S(2)}, u32[]{:S(2)}) %collective-permute-start.5) | collective-permute-done | bytes 196640 | tf_op jit(solution)/shard_map/ppermute | solution.py:375
  57.8 2.4 %add_b.1 = (f32[1024,384]{1,0:T(8,128)S(1)}, f32[1024,128]{1,0:T(8,128)S(1)}, f32[1,128]{1,0:T(1,128)S(1)}) custom-call(s32[1]{0:T(128)} %bitcast.7.my_ref, f32[128,384]{1,0:T(8,128)S(1)} %get-tuple-element.97.refs_0_, f32[128,384]{1,0:T(8,128)S(1)} %collective-permute-done.3.refs_1_, f32[128,384]{1,0:T(8,128)S(1)} %collective-permute-done.4.refs_2_, ...), custom_call_target="tpu_custom_call" | custom-call | flops 21000000 | bytes 1048576 | tf_op jit(solution)/shard_map/add_b/pallas_call | solution.py:434
  60.2 0.0 all-to-all-done.3.a_in
  60.2 5.2 %finish.1 = (f32[1024,768]{1,0:T(8,128)}, f32[1024,768]{1,0:T(8,128)}, f32[1,1]{1,0:T(1,128)}) custom-call(s32[1]{0:T(128)} %bitcast.7.my_ref, f32[8,80,384]{2,1,0:T(8,128)S(1)} %all-to-all-done.3.a_in, f32[1024,384]{1,0:T(8,128)S(1)} %get-tuple-element.101.sum_ref, f32[1024,128]{1,0:T(8,128)S(1)} %get-tuple-element.102.tally_ref, ...), custom_call_target="tpu_custom_call" | custom-call | flops 42000000 | bytes 1048576 | tf_op jit(solution)/shard_map/finish/pallas_call | solution.py:446
  65.4 0.0 copy-done
  65.4 0.8 %while.22 = (f32[]{:T(128)}, f32[1024,768]{1,0:T(8,128)}, f32[1024,768]{1,0:T(8,128)}, s32[512]{0:T(512)S(1)}, f32[512,768]{1,0:T(8,128)}, /*index=5*/s32[512]{0:T(512)S(1)}) while((f32[]{:T(128)}, f32[1024,768]{1,0:T(8,128)}, f32[1024,768]{1,0:T(8,128)}, s32[512]{0:T(512)S(1)}, f32[512,768]{1,0:T(8,128)}, /*index=5*/s32[512]{0:T(512)S(1)}) %tuple.42), condition=%region_10.11_spmd, body=%region_0.10_spmd | while | flops 4857105408 | bytes 42719728 | solution.py:461
  (3 shorter events, 0.0 us)
Async XLA Ops:
  7.0 25.3 %all-to-all-start.4 = ((f32[8,72,384]{2,1,0:T(8,128)}), f32[8,72,384]{2,1,0:T(8,128)S(1)}, u32[]{:S(2)}, u32[]{:S(2)}) async-start(f32[8,72,384]{2,1,0:T(8,128)} %prepare_b.1), calls=%async_computation.4 | async-start | bytes 1769472 | tf_op jit(solution)/shard_map/all_to_all | solution.py:379
  11.5 5.5 %collective-permute-start = (f32[112,384]{1,0:T(8,128)S(1)}, f32[112,384]{1,0:T(8,128)S(1)}, u32[]{:S(2)}, u32[]{:S(2)}) collective-permute-start(f32[112,384]{1,0:T(8,128)S(1)} %get-tuple-element.92), channel_id=1, source_target_pairs={{0,2},{2,4},{4,6},{6,0},{1,3},{3,5},{5,7},{7,1},{8,10},{10,12},{12... | collective-permute-start | bytes 516104 | tf_op jit(solution)/shard_map/ppermute | solution.py:375
  12.8 14.4 %collective-permute-start.1 = (f32[112,384]{1,0:T(8,128)S(1)}, f32[112,384]{1,0:T(8,128)S(1)}, u32[]{:S(2)}, u32[]{:S(2)}) collective-permute-start(f32[112,384]{1,0:T(8,128)S(1)} %get-tuple-element.93), channel_id=1, source_target_pairs={{0,4},{2,6},{4,0},{6,2},{1,5},{3,7},{5,1},{7,3},{8,12},{10,14},{12... | collective-permute-start | bytes 516104 | tf_op jit(solution)/shard_map/ppermute | solution.py:375
  13.8 15.9 %collective-permute-start.2 = (f32[112,384]{1,0:T(8,128)S(1)}, f32[112,384]{1,0:T(8,128)S(1)}, u32[]{:S(2)}, u32[]{:S(2)}) collective-permute-start(f32[112,384]{1,0:T(8,128)S(1)} %get-tuple-element.94), channel_id=1, source_target_pairs={{0,6},{2,0},{4,2},{6,4},{1,7},{3,1},{5,3},{7,5},{8,14},{10,8},{12,... | collective-permute-start | bytes 516104 | tf_op jit(solution)/shard_map/ppermute | solution.py:375
  32.3 33.1 %copy-start = (s32[512]{0:T(512)S(1)}, s32[512]{0:T(512)}, u32[]{:S(2)}) copy-start(s32[512]{0:T(512)} %param.8) | copy-start | bytes 6148
  32.3 33.1 %copy-start.1 = (s32[512]{0:T(512)S(1)}, s32[512]{0:T(512)}, u32[]{:S(2)}) copy-start(s32[512]{0:T(512)} %param.9) | copy-start | bytes 6148
  32.3 27.9 %all-to-all-start.3 = ((f32[8,80,384]{2,1,0:T(8,128)}), f32[8,80,384]{2,1,0:T(8,128)S(1)}, u32[]{:S(2)}, u32[]{:S(2)}) async-start(f32[8,80,384]{2,1,0:T(8,128)} %forward_a.1), calls=%async_computation.3 | async-start | bytes 1966080 | tf_op jit(solution)/shard_map/all_to_all | solution.py:379
  38.3 6.1 %collective-permute-start.3 = (f32[128,384]{1,0:T(8,128)S(1)}, f32[128,384]{1,0:T(8,128)S(1)}, u32[]{:S(2)}, u32[]{:S(2)}) collective-permute-start(f32[128,384]{1,0:T(8,128)S(1)} %get-tuple-element.98), channel_id=1, source_target_pairs={{0,2},{2,4},{4,6},{6,0},{1,3},{3,5},{5,7},{7,1},{8,10},{10,12},{12... | collective-permute-start | bytes 589832 | tf_op jit(solution)/shard_map/ppermute | solution.py:375
  38.4 16.8 %collective-permute-start.4 = (f32[128,384]{1,0:T(8,128)S(1)}, f32[128,384]{1,0:T(8,128)S(1)}, u32[]{:S(2)}, u32[]{:S(2)}) collective-permute-start(f32[128,384]{1,0:T(8,128)S(1)} %get-tuple-element.99), channel_id=1, source_target_pairs={{0,4},{2,6},{4,0},{6,2},{1,5},{3,7},{5,1},{7,3},{8,12},{10,14},{12... | collective-permute-start | bytes 589832 | tf_op jit(solution)/shard_map/ppermute | solution.py:375
  39.8 18.0 %collective-permute-start.5 = (f32[128,384]{1,0:T(8,128)S(1)}, f32[128,384]{1,0:T(8,128)S(1)}, u32[]{:S(2)}, u32[]{:S(2)}) collective-permute-start(f32[128,384]{1,0:T(8,128)S(1)} %get-tuple-element.100), channel_id=1, source_target_pairs={{0,6},{2,0},{4,2},{6,4},{1,7},{3,1},{5,3},{7,5},{8,14},{10,8},{12,... | collective-permute-start | bytes 589832 | tf_op jit(solution)/shard_map/ppermute | solution.py:375

commit v3 on v2

--- a/solution.py
+++ b/solution.py
@@ -13,7 +13,7 @@
 LANES = 128
 F32 = jnp.float32
 BF16 = jnp.bfloat16
-PARTS = 3
+PARTS = 2
 I32 = jnp.int32
 
 
@@ -114,7 +114,13 @@
     for _ in range(PARTS):
         parts.append(x.astype(BF16))
         x = x - parts[-1].astype(F32)
-    return parts
+    return jnp.concatenate(parts, axis=1)
+
+
+def chosen(hot, parts):
+    both = nn_dot(hot, parts)
+    width = both.shape[1] // PARTS
+    return functools.reduce(jnp.add, [both[:, k * width : (k + 1) * width] for k in range(PARTS)])
 
 
 def place(hot):
@@ -140,7 +146,7 @@
     keep = valid & (pos < room - 1)
     slot = jnp.where(keep, group * room + pos, -1)
     pick = as_bf16(iota((groups * room, lanes), 0) == slot)
-    out = functools.reduce(jnp.add, [nn_dot(pick, part) for part in parts])
+    out = chosen(pick, parts)
     w = weight.astype(I32)
     pieces = [
         shift_div(ids, 16384),
@@ -192,18 +198,18 @@
     return jnp.where(most > room - 1, 1.0, 0.0)
 
 
-def gy_shift(gy, me, sizes):
+def split_device(device, sizes):
     _, n_gy, n_gz = sizes
-    return (gy - (shift_div(me, n_gz) & (n_gy - 1)) + n_gy) & (n_gy - 1)
-
-
-def split_owner(ids, sizes):
-    _, n_gy, n_gz = sizes
-    owner = shift_div(ids, CL_DEV)
-    gz = owner & (n_gz - 1)
-    gy = shift_div(owner, n_gz) & (n_gy - 1)
-    gx = shift_div(owner, n_gz * n_gy)
+    gz = device & (n_gz - 1)
+    gy = shift_div(device, n_gz) & (n_gy - 1)
+    gx = shift_div(device, n_gz * n_gy)
     return gy, gx * n_gz + gz
+
+
+def offsets(ids, me, sizes):
+    gy, plane = split_device(shift_div(ids, CL_DEV), sizes)
+    my_gy, my_plane = split_device(me, sizes)
+    return gy ^ my_gy, plane ^ my_plane
 
 
 def prepare_a_kernel(sizes, room, my_ref, x_ref, assign_ref, index_ref, *outs):
@@ -217,10 +223,9 @@
     weight_col = nn_dot(hot, jnp.ones((count_pts, LANES), BF16))
     wide_ref[...] = weight_col
     wide = jnp.concatenate([weight_col] * (half // LANES), axis=1)
-    gy, _ = split_owner(ids, sizes)
-    shift = gy_shift(gy, my_ref[0], sizes)
+    along, _ = offsets(ids, my_ref[0], sizes)
     most = pack(
-        split(x_ref[...] * wide), ids, weight, shift, n_gy, room,
+        split(x_ref[...] * wide), ids, weight, along, n_gy, room,
         lambda g, *v: write_block(a_refs[g], (), room, *v),
     )
     counts = demand(ids, weight)
@@ -228,19 +233,18 @@
         write_news(a_refs[g], (), room, above(most, room), counts)
 
 
-def prepare_b_kernel(sizes, room, x_ref, assign_ref, weight_ref, wide_ref, b_ref):
-    n_gx, _, n_gz = sizes
+def prepare_b_kernel(sizes, room, my_ref, x_ref, assign_ref, weight_ref, wide_ref, *b_refs):
     half = x_ref.shape[1]
     ids, weight = assign_ref[...], weight_ref[...]
     wide = jnp.concatenate([wide_ref[...]] * (half // LANES), axis=1)
-    _, plane = split_owner(ids, sizes)
+    _, across = offsets(ids, my_ref[0], sizes)
     most = pack(
-        split(x_ref[...] * wide), ids, weight, plane, n_gx * n_gz, room,
-        lambda g, *v: write_block(b_ref, (g,), room, *v),
+        split(x_ref[...] * wide), ids, weight, across, len(b_refs), room,
+        lambda g, *v: write_block(b_refs[g], (), room, *v),
     )
     counts = demand(ids, weight)
-    for g in range(n_gx * n_gz):
-        write_news(b_ref, (g,), room, above(most, room), counts)
+    for ref in b_refs:
+        write_news(ref, (), room, above(most, room), counts)
 
 
 def demand(ids, weight):
@@ -270,37 +274,22 @@
     )
 
 
-def forward_b_kernel(sizes, room, my_ref, b_in, *b_out):
-    n_gx, n_gy, n_gz = sizes
-    rows, ids, weight, flag, counts = gathered([b_in[g] for g in range(n_gx * n_gz)])
-    gy, _ = split_owner(ids, sizes)
+def forward_kernel(sizes, room, to_plane, count_in, my_ref, *refs):
+    outs = refs[count_in:]
+    rows, ids, weight, flag, counts = gathered([r[...] for r in refs[:count_in]])
+    along, across = offsets(ids, my_ref[0], sizes)
     pack(
-        split(rows), ids, weight, gy_shift(gy, my_ref[0], sizes), n_gy, room,
-        lambda g, *v: write_block(b_out[g], (), room, *v),
+        split(rows), ids, weight, across if to_plane else along, len(outs), room,
+        lambda g, *v: write_block(outs[g], (), room, *v),
     )
     flag = jnp.maximum(flag, above(jnp.max(counts), room))
-    for g in range(n_gy):
-        write_news(b_out[g], (), room, flag, counts)
-
-
-def forward_a_kernel(sizes, room, *refs):
-    n_gx, n_gy, n_gz = sizes
-    a_in, a_out = refs[:n_gy], refs[n_gy]
-    rows, ids, weight, flag, counts = gathered([r[...] for r in a_in])
-    _, plane = split_owner(ids, sizes)
-    pack(
-        split(rows), ids, weight, plane, n_gx * n_gz, room,
-        lambda g, *v: write_block(a_out, (g,), room, *v),
-    )
-    flag = jnp.maximum(flag, above(jnp.max(counts), room))
-    for g in range(n_gx * n_gz):
-        write_news(a_out, (g,), room, flag, counts)
-
-
-def add_b_kernel(sizes, block, my_ref, *refs):
-    _, n_gy, _ = sizes
-    b_in, sum_ref, tally_ref, flag_ref = refs[:n_gy], refs[n_gy], refs[n_gy + 1], refs[n_gy + 2]
-    rows, ids, weight, flag, _ = gathered([r[...] for r in b_in])
+    for ref in outs:
+        write_news(ref, (), room, flag, counts)
+
+
+def add_kernel(block, my_ref, *refs):
+    blocks, (sum_ref, tally_ref, flag_ref) = refs[:-3], refs[-3:]
+    rows, ids, weight, flag, _ = gathered([r[...] for r in blocks])
     flag_ref[...] = jnp.full((1, LANES), 1.0, F32) * flag
     parts = split(rows)
     w = weight.astype(I32)
@@ -310,33 +299,31 @@
     low = jnp.broadcast_to((w & 127).astype(F32), (LANES, lanes)).astype(BF16)
     for first in range(0, CL_DEV, block):
         hot = as_bf16(iota((block, lanes), 0) + first == target)
-        sum_ref[first : first + block] = functools.reduce(jnp.add, [nn_dot(hot, p) for p in parts])
-        tally_ref[first : first + block] = nt_dot(hot, high) * 128.0 + nt_dot(hot, low)
-
-
-def finish_kernel(
-    sizes, my_ref, a_in, sum_ref, tally_ref, flag_b_ref, means_ref, cent_ref, flag_ref, x_ref, t_ref
-):
-    n_gx, _, n_gz = sizes
+        sum_ref[first : first + block] = chosen(hot, parts)
+        tally = nt_dot(hot, high) * 128.0 + nt_dot(hot, low)
+        tally_ref[first : first + block] = 1.0 / jnp.maximum(tally, 1.0)
+
+
+def finish_kernel(count_in, my_ref, *refs):
+    blocks = refs[:count_in]
+    sum_ref, share_ref, flag_a_ref, means_ref, cent_ref, flag_ref, x_ref, t_ref = refs[count_in:]
     block = means_ref.shape[0]
     half = means_ref.shape[1] // 2
     step = pl.program_id(0)
 
     @pl.when(step == 0)
     def _():
-        rows, ids, weight, flag, _ = gathered([a_in[g] for g in range(n_gx * n_gz)])
-        flag_ref[0, 0] = jnp.maximum(flag, jnp.max(flag_b_ref[...]))
-        for k, part in enumerate(split(rows)):
-            x_ref[k] = part
+        rows, ids, weight, flag, _ = gathered([r[...] for r in blocks])
+        flag_ref[0, 0] = jnp.maximum(flag, jnp.max(flag_a_ref[...]))
+        x_ref[...] = split(rows)
         t_ref[0:1, :] = jnp.where(weight > 0.0, ids - my_ref[0] * CL_DEV, -1)
 
     first = pl.multiple_of(step * block, block)
     lanes = t_ref.shape[1]
     hot = as_bf16(iota((block, lanes), 0) + first == t_ref[0:1, :])
-    left = functools.reduce(jnp.add, [nn_dot(hot, x_ref[k]) for k in range(PARTS)])
-    right = sum_ref[pl.ds(first, block)]
-    share = 1.0 / jnp.maximum(tally_ref[pl.ds(first, block)], 1.0)
-    wide = jnp.concatenate([share] * (half // LANES), axis=1)
+    right = chosen(hot, x_ref[...])
+    left = sum_ref[pl.ds(first, block)]
+    wide = jnp.concatenate([share_ref[pl.ds(first, block)]] * (half // LANES), axis=1)
     left, right = left * wide, right * wide
     square = jnp.sum(left * left + right * right, axis=1, keepdims=True)
     scale = 1.0 / jnp.sqrt(square + 1e-06)
@@ -369,14 +356,11 @@
     my_gx, my_gy, my_gz = (lax.axis_index(a) for a in ("gx", "gy", "gz"))
     me = ((my_gx * n_gy + my_gy) * n_gz + my_gz).astype(I32).reshape(1)
 
-    def along_gy(blocks):
+    def exchange(blocks, axes):
         out = [blocks[0]]
-        for s in range(1, n_gy):
-            out.append(lax.ppermute(blocks[s], "gy", [(i, (i + s) % n_gy) for i in range(n_gy)]))
+        for r in range(1, len(blocks)):
+            out.append(lax.ppermute(blocks[r], axes, [(i, i ^ r) for i in range(len(blocks))]))
         return out
-
-    def in_plane(blocks):
-        return lax.all_to_all(blocks, ("gx", "gz"), split_axis=0, concat_axis=0, tiled=True)
 
     def cost(us):
         return pl.CostEstimate(flops=us * 7_000_000, bytes_accessed=1 << 20, transcendentals=0)
@@ -387,6 +371,7 @@
     def shape(*dims):
         return jax.ShapeDtypeStruct(dims, F32)
 
+    assign = assignment.reshape(1, count_pts)
     assign = assignment.reshape(1, count_pts)
     sent = pl.pallas_call(
         functools.partial(prepare_a_kernel, sizes, room_a1),
@@ -398,62 +383,55 @@
         cost_estimate=cost(3),
         name="prepare_a",
     )(me, points, assign, sample_index.reshape(1, count_pts))
-    a1 = along_gy(sent[:n_gy])
+    a1 = exchange(sent[:n_gy], "gy")
     sent_b = pl.pallas_call(
         functools.partial(prepare_b_kernel, sizes, room_b1),
         grid=(1,),
-        in_specs=[pl.BlockSpec((count_pts, half), lambda i: (0, 1))] + [VMEM_SPEC] * 3,
-        out_specs=VMEM_SPEC,
-        out_shape=shape(n_plane, room_b1, half),
+        in_specs=[SMEM_SPEC, pl.BlockSpec((count_pts, half), lambda i: (0, 1))] + [VMEM_SPEC] * 3,
+        out_specs=[VMEM_SPEC] * n_plane,
+        out_shape=[shape(room_b1, half)] * n_plane,
         compiler_params=vmem(12),
         cost_estimate=cost(3),
         name="prepare_b",
-    )(points, assign, sent[n_gy], sent[n_gy + 1])
-    b1 = in_plane(sent_b)
-    sent_a = pl.pallas_call(
-        functools.partial(forward_a_kernel, sizes, room_a2),
-        in_specs=[VMEM_SPEC] * n_gy,
-        out_specs=VMEM_SPEC,
-        out_shape=shape(n_plane, room_a2, half),
-        compiler_params=vmem(8),
-        cost_estimate=cost(3),
-        name="forward_a",
-    )(*a1)
-    a2 = in_plane(sent_a)
-    sent_b = pl.pallas_call(
-        functools.partial(forward_b_kernel, sizes, room_b2),
-        in_specs=[SMEM_SPEC, VMEM_SPEC],
-        out_specs=[VMEM_SPEC] * n_gy,
-        out_shape=[shape(room_b2, half)] * n_gy,
-        compiler_params=vmem(8),
-        cost_estimate=cost(3),
-        name="forward_b",
-    )(me, b1)
-    b2 = along_gy(sent_b)
-    block = CL_DEV // 4
-    sum_b, tally, flag_b = pl.pallas_call(
-        functools.partial(add_b_kernel, sizes, block),
-        in_specs=[SMEM_SPEC] + [VMEM_SPEC] * n_gy,
+    )(me, points, assign, sent[n_gy], sent[n_gy + 1])
+    b1 = exchange(sent_b, ("gx", "gz"))
+
+    def forward(blocks, to_plane, room):
+        count = n_plane if to_plane else n_gy
+        return pl.pallas_call(
+            functools.partial(forward_kernel, sizes, room, to_plane, len(blocks)),
+            in_specs=[SMEM_SPEC] + [VMEM_SPEC] * len(blocks),
+            out_specs=[VMEM_SPEC] * count,
+            out_shape=[shape(room, half)] * count,
+            compiler_params=vmem(8),
+            cost_estimate=cost(3),
+        )(me, *blocks)
+
+    a2 = exchange(forward(a1, True, room_a2), ("gx", "gz"))
+    b2 = exchange(forward(b1, False, room_b2), "gy")
+    sum_a, share, flag_a = pl.pallas_call(
+        functools.partial(add_kernel, CL_DEV // 4),
+        in_specs=[SMEM_SPEC] + [VMEM_SPEC] * n_plane,
         out_specs=[VMEM_SPEC] * 3,
         out_shape=[shape(CL_DEV, half), shape(CL_DEV, LANES), shape(1, LANES)],
-        compiler_params=vmem(8),
+        compiler_params=vmem(10),
         cost_estimate=cost(3),
-        name="add_b",
-    )(me, *b2)
+        name="add_a",
+    )(me, *a2)
     steps = 4
     block = CL_DEV // steps
-    lanes_a = n_plane * room_a2
+    lanes_b = n_gy * room_b2
     means, centroids, over = pl.pallas_call(
-        functools.partial(finish_kernel, sizes),
+        functools.partial(finish_kernel, n_gy),
         grid=(steps,),
-        in_specs=[SMEM_SPEC] + [VMEM_SPEC] * 4,
+        in_specs=[SMEM_SPEC] + [VMEM_SPEC] * (n_gy + 3),
         out_specs=[pl.BlockSpec((block, features), lambda i: (i, 0))] * 2 + [SMEM_SPEC],
         out_shape=[shape(CL_DEV, features)] * 2 + [shape(1, 1)],
-        scratch_shapes=[pltpu.VMEM((PARTS, lanes_a, half), BF16), pltpu.VMEM((8, lanes_a), I32)],
+        scratch_shapes=[pltpu.VMEM((lanes_b, PARTS * half), BF16), pltpu.VMEM((8, lanes_b), I32)],
         compiler_params=vmem(16, dimension_semantics=("arbitrary",)),
         cost_estimate=cost(6),
         name="finish",
-    )(me, a2, sum_b, tally, flag_b)
+    )(me, *b2, sum_a, share, flag_a)
 
     def again(carry):
         return (jnp.float32(0.0),) + full_body(points, assignment, sample_index)

time: 66.7 us -> 60.9 us (0.913)
  the two profiles are of different devices: /device:TPU:11 before, /device:TPU:0 now
where the time goes in v3:
time: 60.9 us; the launch traced here: 59.7 us
  starting transfers between devices  27.5 us (45%)
  waiting for transfers between devices  17.4 us (29%)
  Pallas kernels  12.9 us (21%)
  between operations  0.91 us (1%)
  loops' own time  0.88 us (1%)
    ppermute x20, starting transfers between devices, exchange(): lax.ppermute(blocks[r], axes, [(i, i ^ r) for i in range(len(blocks))])  27.5 us
    ppermute x20, waiting for transfers between devices, exchange(): lax.ppermute(blocks[r], axes, [(i, i ^ r) for i in range(len(blocks))])  17.4 us
    pallas_call x1, Pallas kernels, body(): pl.pallas_call(functools.partial(finish_kernel, n_gy), grid=(steps,), in_...  3.94 us
    pallas_call x1, Pallas kernels, body(): pl.pallas_call(functools.partial(prepare_a_kernel, sizes, room_a1), grid=...  2.41 us
    pallas_call x2, Pallas kernels, forward(): pl.pallas_call(functools.partial(forward_kernel, sizes, room, to_plane, l...  2.21 us
    pallas_call x1, Pallas kernels, body(): pl.pallas_call(functools.partial(add_kernel, CL_DEV // 4), in_specs=[SMEM...  2.19 us
    pallas_call x1, Pallas kernels, body(): pl.pallas_call(functools.partial(prepare_b_kernel, sizes, room_b1), grid=...  2.18 us
  transfers between devices with their start and end apart: 20, of which 7 were waited for; matrix products, arithmetic and copies ran while one was open for 0% of the time, Pallas kernels for 11%

profile of v3, /device:TPU:0, one launch (start us, length us, event | category | flops | bytes accessed | tf_op | source)
XLA Modules:
  0.0 59.7 jit_solution(14965661405296283871)
XLA Ops:
  0.6 2.4 %prepare_a.1 = (f32[112,384]{1,0:T(8,128)S(1)}, f32[112,384]{1,0:T(8,128)S(1)}, f32[112,384]{1,0:T(8,128)S(1)}, f32[112,384]{1,0:T(8,128)S(1)}, f32[1,512]{1,0:T(1,128)S(1)}, /*index=5*/f32[512,128]{1,0:T(8,128)S(1)}) custom-call(s32[1]{0:T(128)} %bitcast.7.my_ref, f32[512,768]{1,0:T(8,128)} %x_ref.3, s32[1,512]{1,0:T(1,128)} %bitcast.18, s32[1,512]{1,0:T(1,128)} %bitcast.22), custom_call_target="tpu_custom_call" | custom-call | flops 21000000 | bytes 1048576 | tf_op jit(solution)/shard_map/prepare_a/pallas_call | solution.py:376
  3.1 3.1 %collective-permute-start.10 = (f32[112,384]{1,0:T(8,128)S(1)}, f32[112,384]{1,0:T(8,128)S(1)}, u32[]{:S(2)}, u32[]{:S(2)}) collective-permute-start(f32[112,384]{1,0:T(8,128)S(1)} %get-tuple-element.122), channel_id=1, source_target_pairs={{0,2},{2,0},{4,6},{6,4},{1,3},{3,1},{5,7},{7,5},{8,10},{10,8},{12,... | collective-permute-start | bytes 516104 | tf_op jit(solution)/shard_map/ppermute | solution.py:362
  6.2 2.2 %prepare_b.1 = (f32[72,384]{1,0:T(8,128)S(1)}, f32[72,384]{1,0:T(8,128)S(1)}, f32[72,384]{1,0:T(8,128)S(1)}, f32[72,384]{1,0:T(8,128)S(1)}, f32[72,384]{1,0:T(8,...) custom-call(s32[1]{0:T(128)} %bitcast.7.my_ref, f32[512,768]{1,0:T(8,128)} %x_ref.3, ...), custom_call_target="tpu_custom_call" | custom-call | flops 21000000 | bytes 1048576 | tf_op jit(solution)/shard_map/prepare_b/pallas_call | solution.py:387
  8.4 1.6 %collective-permute-start = (f32[72,384]{1,0:T(8,128)S(1)}, f32[72,384]{1,0:T(8,128)S(1)}, u32[]{:S(2)}, u32[]{:S(2)}) collective-permute-start(f32[72,384]{1,0:T(8,128)S(1)} %get-tuple-element.110), channel_id=1, source_target_pairs={{0,1},{1,0},{8,9},{9,8},{16,17},{17,16},{24,25},{25,24},{2,3},{3,2... | collective-permute-start | bytes 331784 | tf_op jit(solution)/shard_map/ppermute | solution.py:362
  10.0 2.6 %collective-permute-start.11 = (f32[112,384]{1,0:T(8,128)S(1)}, f32[112,384]{1,0:T(8,128)S(1)}, u32[]{:S(2)}, u32[]{:S(2)}) collective-permute-start(f32[112,384]{1,0:T(8,128)S(1)} %get-tuple-element.123), channel_id=1, source_target_pairs={{0,4},{2,6},{4,0},{6,2},{1,5},{3,7},{5,1},{7,3},{8,12},{10,14},{12... | collective-permute-start | bytes 516104 | tf_op jit(solution)/shard_map/ppermute | solution.py:362
  13.2 1.5 %collective-permute-start.3 = (f32[72,384]{1,0:T(8,128)S(1)}, f32[72,384]{1,0:T(8,128)S(1)}, u32[]{:S(2)}, u32[]{:S(2)}) collective-permute-start(f32[72,384]{1,0:T(8,128)S(1)} %get-tuple-element.113), channel_id=1, source_target_pairs={{0,16},{1,17},{8,24},{9,25},{16,0},{17,1},{24,8},{25,9},{2,18},{3,... | collective-permute-start | bytes 331784 | tf_op jit(solution)/shard_map/ppermute | solution.py:362
  14.7 1.5 %collective-permute-start.4 = (f32[72,384]{1,0:T(8,128)S(1)}, f32[72,384]{1,0:T(8,128)S(1)}, u32[]{:S(2)}, u32[]{:S(2)}) collective-permute-start(f32[72,384]{1,0:T(8,128)S(1)} %get-tuple-element.114), channel_id=1, source_target_pairs={{0,17},{1,16},{8,25},{9,24},{16,1},{17,0},{24,9},{25,8},{2,19},{3,... | collective-permute-start | bytes 331784 | tf_op jit(solution)/shard_map/ppermute | solution.py:362
  16.2 8.8 %collective-permute-done.11.refs_2_ = f32[112,384]{1,0:T(8,128)S(1)} collective-permute-done((f32[112,384]{1,0:T(8,128)S(1)}, f32[112,384]{1,0:T(8,128)S(1)}, u32[]{:S(2)}, u32[]{:S(2)}) %collective-permute-start.11) | collective-permute-done | bytes 172064 | tf_op jit(solution)/shard_map/ppermute | solution.py:362
  25.0 1.1 %collective-permute-start.5 = (f32[72,384]{1,0:T(8,128)S(1)}, f32[72,384]{1,0:T(8,128)S(1)}, u32[]{:S(2)}, u32[]{:S(2)}) collective-permute-start(f32[72,384]{1,0:T(8,128)S(1)} %get-tuple-element.115), channel_id=1, source_target_pairs={{0,24},{1,25},{8,16},{9,17},{16,8},{17,9},{24,0},{25,1},{2,26},{3,... | collective-permute-start | bytes 331784 | tf_op jit(solution)/shard_map/ppermute | solution.py:362
  26.6 1.1 %shard_map.51 = (f32[80,384]{1,0:T(8,128)S(1)}, f32[80,384]{1,0:T(8,128)S(1)}, f32[80,384]{1,0:T(8,128)S(1)}, f32[80,384]{1,0:T(8,128)S(1)}, f32[80,384]{1,0:T(8...) custom-call(s32[1]{0:T(128)} %bitcast.7.my_ref, ...), custom_call_target="tpu_custom_call" | custom-call | flops 21000000 | bytes 1048576 | tf_op jit(solution)/shard_map/pallas_call | solution.py:401
  27.7 1.7 %collective-permute-start.13 = (f32[80,384]{1,0:T(8,128)S(1)}, f32[80,384]{1,0:T(8,128)S(1)}, u32[]{:S(2)}, u32[]{:S(2)}) collective-permute-start(f32[80,384]{1,0:T(8,128)S(1)} %get-tuple-element.126), channel_id=1, source_target_pairs={{0,1},{1,0},{8,9},{9,8},{16,17},{17,16},{24,25},{25,24},{2,3},{3,2... | collective-permute-start | bytes 368648 | tf_op jit(solution)/shard_map/ppermute | solution.py:362
  30.1 1.5 %collective-permute-start.16 = (f32[80,384]{1,0:T(8,128)S(1)}, f32[80,384]{1,0:T(8,128)S(1)}, u32[]{:S(2)}, u32[]{:S(2)}) collective-permute-start(f32[80,384]{1,0:T(8,128)S(1)} %get-tuple-element.129), channel_id=1, source_target_pairs={{0,16},{1,17},{8,24},{9,25},{16,0},{17,1},{24,8},{25,9},{2,18},{3,... | collective-permute-start | bytes 368648 | tf_op jit(solution)/shard_map/ppermute | solution.py:362
  32.2 2.7 %collective-permute-start.17 = (f32[80,384]{1,0:T(8,128)S(1)}, f32[80,384]{1,0:T(8,128)S(1)}, u32[]{:S(2)}, u32[]{:S(2)}) collective-permute-start(f32[80,384]{1,0:T(8,128)S(1)} %get-tuple-element.130), channel_id=1, source_target_pairs={{0,17},{1,16},{8,25},{9,24},{16,1},{17,0},{24,9},{25,8},{2,19},{3,... | collective-permute-start | bytes 368648 | tf_op jit(solution)/shard_map/ppermute | solution.py:362
  35.0 1.1 %shard_map.50 = (f32[128,384]{1,0:T(8,128)S(1)}, f32[128,384]{1,0:T(8,128)S(1)}, f32[128,384]{1,0:T(8,128)S(1)}, f32[128,384]{1,0:T(8,128)S(1)}) custom-call(s32[1]{0:T(128)} %bitcast.7.my_ref, f32[72,384]{1,0:T(8,128)S(1)} %get-tuple-element.109.refs_0_, f32[72,384]{1,0:T(8,128)S(1)} %collective-permute-done.refs_1_, ...), custom_call_target="tpu_custom_call" | custom-call | flops 21000000 | bytes 1048576 | tf_op jit(solution)/shard_map/pallas_call | solution.py:401
  36.1 2.0 %collective-permute-start.7 = (f32[128,384]{1,0:T(8,128)S(1)}, f32[128,384]{1,0:T(8,128)S(1)}, u32[]{:S(2)}, u32[]{:S(2)}) collective-permute-start(f32[128,384]{1,0:T(8,128)S(1)} %get-tuple-element.118), channel_id=1, source_target_pairs={{0,2},{2,0},{4,6},{6,4},{1,3},{3,1},{5,7},{7,5},{8,10},{10,8},{12,... | collective-permute-start | bytes 589832 | tf_op jit(solution)/shard_map/ppermute | solution.py:362
  38.1 1.2 %collective-permute-start.8 = (f32[128,384]{1,0:T(8,128)S(1)}, f32[128,384]{1,0:T(8,128)S(1)}, u32[]{:S(2)}, u32[]{:S(2)}) collective-permute-start(f32[128,384]{1,0:T(8,128)S(1)} %get-tuple-element.119), channel_id=1, source_target_pairs={{0,4},{2,6},{4,0},{6,2},{1,5},{3,7},{5,1},{7,3},{8,12},{10,14},{12... | collective-permute-start | bytes 589832 | tf_op jit(solution)/shard_map/ppermute | solution.py:362
  39.3 1.0 %collective-permute-done.15.refs_3_ = f32[80,384]{1,0:T(8,128)S(1)} collective-permute-done((f32[80,384]{1,0:T(8,128)S(1)}, f32[80,384]{1,0:T(8,128)S(1)}, u32[]{:S(2)}, u32[]{:S(2)}) %collective-permute-start.15) | collective-permute-done | bytes 122912 | tf_op jit(solution)/shard_map/ppermute | solution.py:362
  40.3 3.1 %collective-permute-start.9 = (f32[128,384]{1,0:T(8,128)S(1)}, f32[128,384]{1,0:T(8,128)S(1)}, u32[]{:S(2)}, u32[]{:S(2)}) collective-permute-start(f32[128,384]{1,0:T(8,128)S(1)} %get-tuple-element.120), channel_id=1, source_target_pairs={{0,6},{2,4},{4,2},{6,0},{1,7},{3,5},{5,3},{7,1},{8,14},{10,12},{12... | collective-permute-start | bytes 589832 | tf_op jit(solution)/shard_map/ppermute | solution.py:362
  43.8 2.3 %collective-permute-start.19 = (f32[80,384]{1,0:T(8,128)S(1)}, f32[80,384]{1,0:T(8,128)S(1)}, u32[]{:S(2)}, u32[]{:S(2)}) collective-permute-start(f32[80,384]{1,0:T(8,128)S(1)} %get-tuple-element.132), channel_id=1, source_target_pairs={{0,25},{1,24},{8,17},{9,16},{16,9},{17,8},{24,1},{25,0},{2,27},{3,... | collective-permute-start | bytes 368648 | tf_op jit(solution)/shard_map/ppermute | solution.py:362
  46.1 2.8 %collective-permute-done.18.refs_6_ = f32[80,384]{1,0:T(8,128)S(1)} collective-permute-done((f32[80,384]{1,0:T(8,128)S(1)}, f32[80,384]{1,0:T(8,128)S(1)}, u32[]{:S(2)}, u32[]{:S(2)}) %collective-permute-start.18) | collective-permute-done | bytes 122912 | tf_op jit(solution)/shard_map/ppermute | solution.py:362
  48.9 3.5 %collective-permute-done.19.refs_7_ = f32[80,384]{1,0:T(8,128)S(1)} collective-permute-done((f32[80,384]{1,0:T(8,128)S(1)}, f32[80,384]{1,0:T(8,128)S(1)}, u32[]{:S(2)}, u32[]{:S(2)}) %collective-permute-start.19) | collective-permute-done | bytes 122912 | tf_op jit(solution)/shard_map/ppermute | solution.py:362
  52.5 2.2 %add_a.1 = (f32[1024,384]{1,0:T(8,128)S(1)}, f32[1024,128]{1,0:T(8,128)S(1)}, f32[1,128]{1,0:T(1,128)S(1)}) custom-call(s32[1]{0:T(128)} %bitcast.7.my_ref, f32[80,384]{1,0:T(8,128)S(1)} %get-tuple-element.125.refs_0_, f32[80,384]{1,0:T(8,128)S(1)} %collective-permute-done.13.refs_1_, f32[80,384]{1,0:T(8,128)S(1)} %collective-permute-done.14.refs_2_, ...), custom_call_target="tpu_custom_call" | custom-call | flops 21000000 | bytes 1048576 | tf_op jit(solution)/shard_map/add_a/pallas_call | solution.py:412
  54.7 3.9 %finish.1 = (f32[1024,768]{1,0:T(8,128)}, f32[1024,768]{1,0:T(8,128)}, f32[1,1]{1,0:T(1,128)}) custom-call(s32[1]{0:T(128)} %bitcast.7.my_ref, f32[128,384]{1,0:T(8,128)S(1)} %get-tuple-element.117.refs_0_, f32[128,384]{1,0:T(8,128)S(1)} %collective-permute-done.7.refs_1_, f32[128,384]{1,0:T(8,128)S(1)} %collective-permute-done.8.refs_2_, ...), custom_call_target="tpu_custom_call" | custom-call | flops 42000000 | bytes 1048576 | tf_op jit(solution)/shard_map/finish/pallas_call | solution.py:424
  58.7 0.9 %while.22 = (f32[]{:T(128)}, f32[1024,768]{1,0:T(8,128)}, f32[1024,768]{1,0:T(8,128)}, s32[512]{0:T(512)S(1)}, f32[512,768]{1,0:T(8,128)S(1)}, /*index=5*/s32[512]{0:T(512)S(1)}) while((f32[]{:T(128)}, f32[1024,768]{1,0:T(8,128)}, f32[1024,768]{1,0:T(8,128)}, s32[512]{0:T(512)S(1)}, f32[512,768]{1,0:T(8,128)S(1)}, /*index=5*/s32[512]{0:T(512)S(1)}) %tuple.43), condition=%region_10.11_spmd, body=%region_0.10_spmd | while | flops 4857105408 | bytes 55302668 | solution.py:439
  (29 shorter events, 3.0 us)
Async XLA Ops:
  3.1 11.7 %collective-permute-start.10 = (f32[112,384]{1,0:T(8,128)S(1)}, f32[112,384]{1,0:T(8,128)S(1)}, u32[]{:S(2)}, u32[]{:S(2)}) collective-permute-start(f32[112,384]{1,0:T(8,128)S(1)} %get-tuple-element.122), channel_id=1, source_target_pairs={{0,2},{2,0},{4,6},{6,4},{1,3},{3,1},{5,7},{7,5},{8,10},{10,8},{12,... | collective-permute-start | bytes 516104 | tf_op jit(solution)/shard_map/ppermute | solution.py:362
  8.4 50.3 %copy-start = (f32[512,768]{1,0:T(8,128)S(1)}, f32[512,768]{1,0:T(8,128)}, u32[]{:S(2)}) copy-start(f32[512,768]{1,0:T(8,128)} %x_ref.3) | copy-start | bytes 4718596
  8.4 50.3 %copy-start.2 = (s32[512]{0:T(512)S(1)}, s32[512]{0:T(512)}, u32[]{:S(2)}) copy-start(s32[512]{0:T(512)} %param.8) | copy-start | bytes 6148
  8.4 50.3 %copy-start.3 = (s32[512]{0:T(512)S(1)}, s32[512]{0:T(512)}, u32[]{:S(2)}) copy-start(s32[512]{0:T(512)} %param.9) | copy-start | bytes 6148
  8.4 4.8 %collective-permute-start = (f32[72,384]{1,0:T(8,128)S(1)}, f32[72,384]{1,0:T(8,128)S(1)}, u32[]{:S(2)}, u32[]{:S(2)}) collective-permute-start(f32[72,384]{1,0:T(8,128)S(1)} %get-tuple-element.110), channel_id=1, source_target_pairs={{0,1},{1,0},{8,9},{9,8},{16,17},{17,16},{24,25},{25,24},{2,3},{3,2... | collective-permute-start | bytes 331784 | tf_op jit(solution)/shard_map/ppermute | solution.py:362
  10.0 3.2 %collective-permute-start.1 = (f32[72,384]{1,0:T(8,128)S(1)}, f32[72,384]{1,0:T(8,128)S(1)}, u32[]{:S(2)}, u32[]{:S(2)}) collective-permute-start(f32[72,384]{1,0:T(8,128)S(1)} %get-tuple-element.111), channel_id=1, source_target_pairs={{0,8},{1,9},{8,0},{9,1},{16,24},{17,25},{24,16},{25,17},{2,10},{3,... | collective-permute-start | bytes 331784 | tf_op jit(solution)/shard_map/ppermute | solution.py:362
  10.0 15.0 %collective-permute-start.11 = (f32[112,384]{1,0:T(8,128)S(1)}, f32[112,384]{1,0:T(8,128)S(1)}, u32[]{:S(2)}, u32[]{:S(2)}) collective-permute-start(f32[112,384]{1,0:T(8,128)S(1)} %get-tuple-element.123), channel_id=1, source_target_pairs={{0,4},{2,6},{4,0},{6,2},{1,5},{3,7},{5,1},{7,3},{8,12},{10,14},{12... | collective-permute-start | bytes 516104 | tf_op jit(solution)/shard_map/ppermute | solution.py:362
  12.5 13.5 %collective-permute-start.12 = (f32[112,384]{1,0:T(8,128)S(1)}, f32[112,384]{1,0:T(8,128)S(1)}, u32[]{:S(2)}, u32[]{:S(2)}) collective-permute-start(f32[112,384]{1,0:T(8,128)S(1)} %get-tuple-element.124), channel_id=1, source_target_pairs={{0,6},{2,4},{4,2},{6,0},{1,7},{3,5},{5,3},{7,1},{8,14},{10,12},{12... | collective-permute-start | bytes 516104 | tf_op jit(solution)/shard_map/ppermute | solution.py:362
  13.2 14.4 %collective-permute-start.2 = (f32[72,384]{1,0:T(8,128)S(1)}, f32[72,384]{1,0:T(8,128)S(1)}, u32[]{:S(2)}, u32[]{:S(2)}) collective-permute-start(f32[72,384]{1,0:T(8,128)S(1)} %get-tuple-element.112), channel_id=1, source_target_pairs={{0,9},{1,8},{8,1},{9,0},{16,25},{17,24},{24,17},{25,16},{2,11},{3,... | collective-permute-start | bytes 331784 | tf_op jit(solution)/shard_map/ppermute | solution.py:362
  13.2 16.1 %collective-permute-start.3 = (f32[72,384]{1,0:T(8,128)S(1)}, f32[72,384]{1,0:T(8,128)S(1)}, u32[]{:S(2)}, u32[]{:S(2)}) collective-permute-start(f32[72,384]{1,0:T(8,128)S(1)} %get-tuple-element.113), channel_id=1, source_target_pairs={{0,16},{1,17},{8,24},{9,25},{16,0},{17,1},{24,8},{25,9},{2,18},{3,... | collective-permute-start | bytes 331784 | tf_op jit(solution)/shard_map/ppermute | solution.py:362
  14.7 14.6 %collective-permute-start.4 = (f32[72,384]{1,0:T(8,128)S(1)}, f32[72,384]{1,0:T(8,128)S(1)}, u32[]{:S(2)}, u32[]{:S(2)}) collective-permute-start(f32[72,384]{1,0:T(8,128)S(1)} %get-tuple-element.114), channel_id=1, source_target_pairs={{0,17},{1,16},{8,25},{9,24},{16,1},{17,0},{24,9},{25,8},{2,19},{3,... | collective-permute-start | bytes 331784 | tf_op jit(solution)/shard_map/ppermute | solution.py:362
  25.0 5.1 %collective-permute-start.5 = (f32[72,384]{1,0:T(8,128)S(1)}, f32[72,384]{1,0:T(8,128)S(1)}, u32[]{:S(2)}, u32[]{:S(2)}) collective-permute-start(f32[72,384]{1,0:T(8,128)S(1)} %get-tuple-element.115), channel_id=1, source_target_pairs={{0,24},{1,25},{8,16},{9,17},{16,8},{17,9},{24,0},{25,1},{2,26},{3,... | collective-permute-start | bytes 331784 | tf_op jit(solution)/shard_map/ppermute | solution.py:362
  26.1 6.1 %collective-permute-start.6 = (f32[72,384]{1,0:T(8,128)S(1)}, f32[72,384]{1,0:T(8,128)S(1)}, u32[]{:S(2)}, u32[]{:S(2)}) collective-permute-start(f32[72,384]{1,0:T(8,128)S(1)} %get-tuple-element.116), channel_id=1, source_target_pairs={{0,25},{1,24},{8,17},{9,16},{16,9},{17,8},{24,1},{25,0},{2,27},{3,... | collective-permute-start | bytes 331784 | tf_op jit(solution)/shard_map/ppermute | solution.py:362
  27.7 8.4 %collective-permute-start.13 = (f32[80,384]{1,0:T(8,128)S(1)}, f32[80,384]{1,0:T(8,128)S(1)}, u32[]{:S(2)}, u32[]{:S(2)}) collective-permute-start(f32[80,384]{1,0:T(8,128)S(1)} %get-tuple-element.126), channel_id=1, source_target_pairs={{0,1},{1,0},{8,9},{9,8},{16,17},{17,16},{24,25},{25,24},{2,3},{3,2... | collective-permute-start | bytes 368648 | tf_op jit(solution)/shard_map/ppermute | solution.py:362
  29.3 8.8 %collective-permute-start.14 = (f32[80,384]{1,0:T(8,128)S(1)}, f32[80,384]{1,0:T(8,128)S(1)}, u32[]{:S(2)}, u32[]{:S(2)}) collective-permute-start(f32[80,384]{1,0:T(8,128)S(1)} %get-tuple-element.127), channel_id=1, source_target_pairs={{0,8},{1,9},{8,0},{9,1},{16,24},{17,25},{24,16},{25,17},{2,10},{3,... | collective-permute-start | bytes 368648 | tf_op jit(solution)/shard_map/ppermute | solution.py:362
  29.3 11.0 %collective-permute-start.15 = (f32[80,384]{1,0:T(8,128)S(1)}, f32[80,384]{1,0:T(8,128)S(1)}, u32[]{:S(2)}, u32[]{:S(2)}) collective-permute-start(f32[80,384]{1,0:T(8,128)S(1)} %get-tuple-element.128), channel_id=1, source_target_pairs={{0,9},{1,8},{8,1},{9,0},{16,25},{17,24},{24,17},{25,16},{2,11},{3,... | collective-permute-start | bytes 368648 | tf_op jit(solution)/shard_map/ppermute | solution.py:362
  30.1 13.3 %collective-permute-start.16 = (f32[80,384]{1,0:T(8,128)S(1)}, f32[80,384]{1,0:T(8,128)S(1)}, u32[]{:S(2)}, u32[]{:S(2)}) collective-permute-start(f32[80,384]{1,0:T(8,128)S(1)} %get-tuple-element.129), channel_id=1, source_target_pairs={{0,16},{1,17},{8,24},{9,25},{16,0},{17,1},{24,8},{25,9},{2,18},{3,... | collective-permute-start | bytes 368648 | tf_op jit(solution)/shard_map/ppermute | solution.py:362
  32.2 11.6 %collective-permute-start.17 = (f32[80,384]{1,0:T(8,128)S(1)}, f32[80,384]{1,0:T(8,128)S(1)}, u32[]{:S(2)}, u32[]{:S(2)}) collective-permute-start(f32[80,384]{1,0:T(8,128)S(1)} %get-tuple-element.130), channel_id=1, source_target_pairs={{0,17},{1,16},{8,25},{9,24},{16,1},{17,0},{24,9},{25,8},{2,19},{3,... | collective-permute-start | bytes 368648 | tf_op jit(solution)/shard_map/ppermute | solution.py:362
  36.1 18.6 %collective-permute-start.7 = (f32[128,384]{1,0:T(8,128)S(1)}, f32[128,384]{1,0:T(8,128)S(1)}, u32[]{:S(2)}, u32[]{:S(2)}) collective-permute-start(f32[128,384]{1,0:T(8,128)S(1)} %get-tuple-element.118), channel_id=1, source_target_pairs={{0,2},{2,0},{4,6},{6,4},{1,3},{3,1},{5,7},{7,5},{8,10},{10,8},{12,... | collective-permute-start | bytes 589832 | tf_op jit(solution)/shard_map/ppermute | solution.py:362
  38.1 16.6 %collective-permute-start.8 = (f32[128,384]{1,0:T(8,128)S(1)}, f32[128,384]{1,0:T(8,128)S(1)}, u32[]{:S(2)}, u32[]{:S(2)}) collective-permute-start(f32[128,384]{1,0:T(8,128)S(1)} %get-tuple-element.119), channel_id=1, source_target_pairs={{0,4},{2,6},{4,0},{6,2},{1,5},{3,7},{5,1},{7,3},{8,12},{10,14},{12... | collective-permute-start | bytes 589832 | tf_op jit(solution)/shard_map/ppermute | solution.py:362
  40.3 14.4 %collective-permute-start.9 = (f32[128,384]{1,0:T(8,128)S(1)}, f32[128,384]{1,0:T(8,128)S(1)}, u32[]{:S(2)}, u32[]{:S(2)}) collective-permute-start(f32[128,384]{1,0:T(8,128)S(1)} %get-tuple-element.120), channel_id=1, source_target_pairs={{0,6},{2,4},{4,2},{6,0},{1,7},{3,5},{5,3},{7,1},{8,14},{10,12},{12... | collective-permute-start | bytes 589832 | tf_op jit(solution)/shard_map/ppermute | solution.py:362
  43.4 5.5 %collective-permute-start.18 = (f32[80,384]{1,0:T(8,128)S(1)}, f32[80,384]{1,0:T(8,128)S(1)}, u32[]{:S(2)}, u32[]{:S(2)}) collective-permute-start(f32[80,384]{1,0:T(8,128)S(1)} %get-tuple-element.131), channel_id=1, source_target_pairs={{0,24},{1,25},{8,16},{9,17},{16,8},{17,9},{24,0},{25,1},{2,26},{3,... | collective-permute-start | bytes 368648 | tf_op jit(solution)/shard_map/ppermute | solution.py:362
  43.8 8.7 %collective-permute-start.19 = (f32[80,384]{1,0:T(8,128)S(1)}, f32[80,384]{1,0:T(8,128)S(1)}, u32[]{:S(2)}, u32[]{:S(2)}) collective-permute-start(f32[80,384]{1,0:T(8,128)S(1)} %get-tuple-element.132), channel_id=1, source_target_pairs={{0,25},{1,24},{8,17},{9,16},{16,9},{17,8},{24,1},{25,0},{2,27},{3,... | collective-permute-start | bytes 368648 | tf_op jit(solution)/shard_map/ppermute | solution.py:362

commit v4 on v3

--- a/solution.py
+++ b/solution.py
@@ -212,39 +212,27 @@
     return gy ^ my_gy, plane ^ my_plane
 
 
-def prepare_a_kernel(sizes, room, my_ref, x_ref, assign_ref, index_ref, *outs):
+def prepare_kernel(sizes, rooms, my_ref, points_ref, assign_ref, index_ref, *outs):
     _, n_gy, _ = sizes
-    a_refs, weight_ref, wide_ref = outs[:n_gy], outs[n_gy], outs[n_gy + 1]
-    count_pts, half = x_ref.shape
+    a_refs, b_refs = outs[:n_gy], outs[n_gy:]
+    count_pts = points_ref.shape[0]
+    half = points_ref.shape[1] // 2
     ids = assign_ref[...]
     hot = as_bf16(iota((count_pts, count_pts), 0) == index_ref[...])
     weight = nt_dot(jnp.ones((8, count_pts), BF16), hot)[0:1]
-    weight_ref[...] = weight
-    weight_col = nn_dot(hot, jnp.ones((count_pts, LANES), BF16))
-    wide_ref[...] = weight_col
-    wide = jnp.concatenate([weight_col] * (half // LANES), axis=1)
-    along, _ = offsets(ids, my_ref[0], sizes)
-    most = pack(
-        split(x_ref[...] * wide), ids, weight, along, n_gy, room,
-        lambda g, *v: write_block(a_refs[g], (), room, *v),
-    )
+    wide = jnp.concatenate([nn_dot(hot, jnp.ones((count_pts, LANES), BF16))] * (half // LANES), axis=1)
+    along, across = offsets(ids, my_ref[0], sizes)
     counts = demand(ids, weight)
-    for g in range(n_gy):
-        write_news(a_refs[g], (), room, above(most, room), counts)
-
-
-def prepare_b_kernel(sizes, room, my_ref, x_ref, assign_ref, weight_ref, wide_ref, *b_refs):
-    half = x_ref.shape[1]
-    ids, weight = assign_ref[...], weight_ref[...]
-    wide = jnp.concatenate([wide_ref[...]] * (half // LANES), axis=1)
-    _, across = offsets(ids, my_ref[0], sizes)
-    most = pack(
-        split(x_ref[...] * wide), ids, weight, across, len(b_refs), room,
-        lambda g, *v: write_block(b_refs[g], (), room, *v),
-    )
-    counts = demand(ids, weight)
-    for ref in b_refs:
-        write_news(ref, (), room, above(most, room), counts)
+    for refs, room, group, columns in (
+        (a_refs, rooms[0], along, slice(0, half)),
+        (b_refs, rooms[1], across, slice(half, 2 * half)),
+    ):
+        most = pack(
+            split(points_ref[:, columns] * wide), ids, weight, group, len(refs), room,
+            lambda g, *v: write_block(refs[g], (), room, *v),
+        )
+        for ref in refs:
+            write_news(ref, (), room, above(most, room), counts)
 
 
 def demand(ids, weight):
@@ -287,50 +275,43 @@
         write_news(ref, (), room, flag, counts)
 
 
-def add_kernel(block, my_ref, *refs):
-    blocks, (sum_ref, tally_ref, flag_ref) = refs[:-3], refs[-3:]
-    rows, ids, weight, flag, _ = gathered([r[...] for r in blocks])
-    flag_ref[...] = jnp.full((1, LANES), 1.0, F32) * flag
-    parts = split(rows)
-    w = weight.astype(I32)
-    target = jnp.where(w > 0, ids - my_ref[0] * CL_DEV, -1)
-    lanes = target.shape[1]
-    high = jnp.broadcast_to(shift_div(w, 128).astype(F32), (LANES, lanes)).astype(BF16)
-    low = jnp.broadcast_to((w & 127).astype(F32), (LANES, lanes)).astype(BF16)
-    for first in range(0, CL_DEV, block):
-        hot = as_bf16(iota((block, lanes), 0) + first == target)
-        sum_ref[first : first + block] = chosen(hot, parts)
-        tally = nt_dot(hot, high) * 128.0 + nt_dot(hot, low)
-        tally_ref[first : first + block] = 1.0 / jnp.maximum(tally, 1.0)
-
-
-def finish_kernel(count_in, my_ref, *refs):
-    blocks = refs[:count_in]
-    sum_ref, share_ref, flag_a_ref, means_ref, cent_ref, flag_ref, x_ref, t_ref = refs[count_in:]
+def finish_kernel(counts_in, my_ref, *refs):
+    count_a, count_b = counts_in
+    a_in, b_in = refs[:count_a], refs[count_a : count_a + count_b]
+    means_ref, cent_ref, flag_ref, xa_ref, xb_ref, ta_ref, tb_ref = refs[count_a + count_b :]
     block = means_ref.shape[0]
-    half = means_ref.shape[1] // 2
     step = pl.program_id(0)
 
     @pl.when(step == 0)
     def _():
-        rows, ids, weight, flag, _ = gathered([r[...] for r in blocks])
-        flag_ref[0, 0] = jnp.maximum(flag, jnp.max(flag_a_ref[...]))
-        x_ref[...] = split(rows)
-        t_ref[0:1, :] = jnp.where(weight > 0.0, ids - my_ref[0] * CL_DEV, -1)
-
-    first = pl.multiple_of(step * block, block)
-    lanes = t_ref.shape[1]
-    hot = as_bf16(iota((block, lanes), 0) + first == t_ref[0:1, :])
-    right = chosen(hot, x_ref[...])
-    left = sum_ref[pl.ds(first, block)]
-    wide = jnp.concatenate([share_ref[pl.ds(first, block)]] * (half // LANES), axis=1)
-    left, right = left * wide, right * wide
-    square = jnp.sum(left * left + right * right, axis=1, keepdims=True)
+        flags = []
+        for blocks, x_ref, t_ref in ((a_in, xa_ref, ta_ref), (b_in, xb_ref, tb_ref)):
+            rows, ids, weight, flag, _ = gathered([r[...] for r in blocks])
+            flags.append(flag)
+            x_ref[...] = split(rows)
+            t_ref[0:1, :] = jnp.where(weight > 0.0, ids - my_ref[0] * CL_DEV, -1)
+            t_ref[1:2, :] = weight.astype(I32)
+        flag_ref[0, 0] = jnp.where(jnp.maximum(flags[0], flags[1]) > 0.0, 1, 0)
+
+    first = step * block
+    sums = []
+    for x_ref, t_ref in ((xa_ref, ta_ref), (xb_ref, tb_ref)):
+        hot = as_bf16(iota((block, t_ref.shape[1]), 0) + first == t_ref[0:1, :])
+        sums.append(chosen(hot, x_ref[...]))
+    w = tb_ref[1:2, :]
+    lanes = w.shape[1]
+    high = jnp.broadcast_to(shift_div(w, 128).astype(F32), (LANES, lanes))
+    low = jnp.broadcast_to((w & 127).astype(F32), (LANES, lanes))
+    pair = nt_dot(hot, jnp.concatenate([high, low], axis=0).astype(BF16))
+    share = 1.0 / jnp.maximum(pair[:, :LANES] * 128.0 + pair[:, LANES:], 1.0)
+    left, right = [x * jnp.concatenate([share] * (x.shape[1] // LANES), axis=1) for x in sums]
+    square = jnp.sum(left * left, axis=1, keepdims=True) + jnp.sum(right * right, axis=1, keepdims=True)
     scale = 1.0 / jnp.sqrt(square + 1e-06)
-    means_ref[:, :half] = left
-    means_ref[:, half:] = right
-    cent_ref[:, :half] = left * scale
-    cent_ref[:, half:] = right * scale
+    width_a = left.shape[1]
+    means_ref[:, :width_a] = left
+    means_ref[:, width_a:] = right
+    cent_ref[:, :width_a] = left * scale
+    cent_ref[:, width_a:] = right * scale
 
 
 VMEM_SPEC = pl.BlockSpec(memory_space=pltpu.VMEM)
@@ -374,27 +355,16 @@
     assign = assignment.reshape(1, count_pts)
     assign = assignment.reshape(1, count_pts)
     sent = pl.pallas_call(
-        functools.partial(prepare_a_kernel, sizes, room_a1),
-        grid=(1,),
-        in_specs=[SMEM_SPEC, pl.BlockSpec((count_pts, half), lambda i: (0, 0))] + [VMEM_SPEC] * 2,
-        out_specs=[VMEM_SPEC] * (n_gy + 2),
-        out_shape=[shape(room_a1, half)] * n_gy + [shape(1, count_pts), shape(count_pts, LANES)],
+        functools.partial(prepare_kernel, sizes, (room_a1, room_b1)),
+        in_specs=[SMEM_SPEC] + [VMEM_SPEC] * 3,
+        out_specs=[VMEM_SPEC] * (n_gy + n_plane),
+        out_shape=[shape(room_a1, half)] * n_gy + [shape(room_b1, half)] * n_plane,
         compiler_params=vmem(12),
-        cost_estimate=cost(3),
-        name="prepare_a",
-    )(me, points, assign, sample_index.reshape(1, count_pts))
+        cost_estimate=cost(5),
+        name="prepare",
+    )(me, points, assignment.reshape(1, count_pts), sample_index.reshape(1, count_pts))
     a1 = exchange(sent[:n_gy], "gy")
-    sent_b = pl.pallas_call(
-        functools.partial(prepare_b_kernel, sizes, room_b1),
-        grid=(1,),
-        in_specs=[SMEM_SPEC, pl.BlockSpec((count_pts, half), lambda i: (0, 1))] + [VMEM_SPEC] * 3,
-        out_specs=[VMEM_SPEC] * n_plane,
-        out_shape=[shape(room_b1, half)] * n_plane,
-        compiler_params=vmem(12),
-        cost_estimate=cost(3),
-        name="prepare_b",
-    )(me, points, assign, sent[n_gy], sent[n_gy + 1])
-    b1 = exchange(sent_b, ("gx", "gz"))
+    b1 = exchange(sent[n_gy:], ("gx", "gz"))
 
     def forward(blocks, to_plane, room):
         count = n_plane if to_plane else n_gy
@@ -409,34 +379,30 @@
 
     a2 = exchange(forward(a1, True, room_a2), ("gx", "gz"))
     b2 = exchange(forward(b1, False, room_b2), "gy")
-    sum_a, share, flag_a = pl.pallas_call(
-        functools.partial(add_kernel, CL_DEV // 4),
-        in_specs=[SMEM_SPEC] + [VMEM_SPEC] * n_plane,
-        out_specs=[VMEM_SPEC] * 3,
-        out_shape=[shape(CL_DEV, half), shape(CL_DEV, LANES), shape(1, LANES)],
-        compiler_params=vmem(10),
-        cost_estimate=cost(3),
-        name="add_a",
-    )(me, *a2)
     steps = 4
     block = CL_DEV // steps
-    lanes_b = n_gy * room_b2
+    lanes_a, lanes_b = n_plane * room_a2, n_gy * room_b2
     means, centroids, over = pl.pallas_call(
-        functools.partial(finish_kernel, n_gy),
+        functools.partial(finish_kernel, (n_plane, n_gy)),
         grid=(steps,),
-        in_specs=[SMEM_SPEC] + [VMEM_SPEC] * (n_gy + 3),
+        in_specs=[SMEM_SPEC] + [VMEM_SPEC] * (n_plane + n_gy),
         out_specs=[pl.BlockSpec((block, features), lambda i: (i, 0))] * 2 + [SMEM_SPEC],
-        out_shape=[shape(CL_DEV, features)] * 2 + [shape(1, 1)],
-        scratch_shapes=[pltpu.VMEM((lanes_b, PARTS * half), BF16), pltpu.VMEM((8, lanes_b), I32)],
-        compiler_params=vmem(16, dimension_semantics=("arbitrary",)),
+        out_shape=[shape(CL_DEV, features)] * 2 + [jax.ShapeDtypeStruct((1, 1), I32)],
+        scratch_shapes=[
+            pltpu.VMEM((lanes_a, PARTS * half), BF16),
+            pltpu.VMEM((lanes_b, PARTS * half), BF16),
+            pltpu.VMEM((8, lanes_a), I32),
+            pltpu.VMEM((8, lanes_b), I32),
+        ],
+        compiler_params=vmem(18, dimension_semantics=("arbitrary",)),
         cost_estimate=cost(6),
         name="finish",
-    )(me, *b2, sum_a, share, flag_a)
+    )(me, *a2, *b2)
 
     def again(carry):
-        return (jnp.float32(0.0),) + full_body(points, assignment, sample_index)
-
-    return lax.while_loop(lambda carry: carry[0] > 0.0, again, (over[0, 0], means, centroids))[1:]
+        return (jnp.int32(0),) + full_body(points, assignment, sample_index)
+
+    return lax.while_loop(lambda carry: carry[0] > 0, again, (over[0, 0], means, centroids))[1:]
 
 
 def solution(mesh):

time: 60.9 us -> 61.2 us (level)
  waiting for transfers between devices: 17.4 us -> 20.9 us
  Pallas kernels: 12.9 us -> 11 us
  starting transfers between devices: 27.5 us -> 26.4 us
    ppermute x20, waiting for transfers between devices: 17.4 us -> 20.9 us  [exchange(): lax.ppermute(blocks[r], axes, [(i, i ^ r) for i in range(len(blocks))])]
    pallas_call x4 -> x2, Pallas kernels: 10.7 us -> 8.79 us  [the longest x1 5.28 us: body(): pl.pallas_call(functools.partial(finish_kernel, (n_plane, n_gy)), grid=(s...]
    ppermute x20, starting transfers between devices: 27.5 us -> 26.4 us  [exchange(): lax.ppermute(blocks[r], axes, [(i, i ^ r) for i in range(len(blocks))])]
  transfers between devices with their start and end apart: 20 -> 20, of which waited for: 7 -> 7; matrix products, arithmetic and copies ran while one was open for 0% -> 0% of each run, Pallas kernels for 11% -> 4%
where the time goes in v4:
time: 61.2 us; the launch traced here: 60 us
  starting transfers between devices  26.4 us (43%)
  waiting for transfers between devices  20.9 us (34%)
  Pallas kernels  11 us (18%)
  loops' own time  0.88 us (1%)
  between operations  0.87 us (1%)
    ppermute x20, starting transfers between devices, exchange(): lax.ppermute(blocks[r], axes, [(i, i ^ r) for i in range(len(blocks))])  26.4 us
    ppermute x20, waiting for transfers between devices, exchange(): lax.ppermute(blocks[r], axes, [(i, i ^ r) for i in range(len(blocks))])  20.9 us
    pallas_call x1, Pallas kernels, body(): pl.pallas_call(functools.partial(finish_kernel, (n_plane, n_gy)), grid=(s...  5.28 us
    pallas_call x1, Pallas kernels, body(): pl.pallas_call(functools.partial(prepare_kernel, sizes, (room_a1, room_b1...  3.51 us
    pallas_call x2, Pallas kernels, forward(): pl.pallas_call(functools.partial(forward_kernel, sizes, room, to_plane, l...  2.21 us
  transfers between devices with their start and end apart: 20, of which 7 were waited for; matrix products, arithmetic and copies ran while one was open for 0% of the time, Pallas kernels for 4%

profile of v4, /device:TPU:0, one launch (start us, length us, event | category | flops | bytes accessed | tf_op | source)
XLA Modules:
  0.0 60.0 jit_solution(6834345410235114997)
XLA Ops:
  0.7 3.5 %prepare.1 = (f32[112,384]{1,0:T(8,128)S(1)}, f32[112,384]{1,0:T(8,128)S(1)}, f32[112,384]{1,0:T(8,128)S(1)}, f32[112,384]{1,0:T(8,128)S(1)}, f32[72,384]{1,0:T(...) custom-call(s32[1]{0:T(128)} %bitcast.7.my_ref, ...), custom_call_target="tpu_custom_call" | custom-call | flops 35000000 | bytes 1048576 | tf_op jit(solution)/shard_map/prepare/pallas_call | solution.py:357
  4.2 3.1 %collective-permute-start = (f32[112,384]{1,0:T(8,128)S(1)}, f32[112,384]{1,0:T(8,128)S(1)}, u32[]{:S(2)}, u32[]{:S(2)}) collective-permute-start(f32[112,384]{1,0:T(8,128)S(1)} %get-tuple-element.103), channel_id=1, source_target_pairs={{0,2},{2,0},{4,6},{6,4},{1,3},{3,1},{5,7},{7,5},{8,10},{10,8},{12,... | collective-permute-start | bytes 516104 | tf_op jit(solution)/shard_map/ppermute | solution.py:343
  7.3 1.5 %collective-permute-start.10 = (f32[72,384]{1,0:T(8,128)S(1)}, f32[72,384]{1,0:T(8,128)S(1)}, u32[]{:S(2)}, u32[]{:S(2)}) collective-permute-start(f32[72,384]{1,0:T(8,128)S(1)} %get-tuple-element.115), channel_id=1, source_target_pairs={{0,1},{1,0},{8,9},{9,8},{16,17},{17,16},{24,25},{25,24},{2,3},{3,2... | collective-permute-start | bytes 331784 | tf_op jit(solution)/shard_map/ppermute | solution.py:343
  8.8 2.6 %collective-permute-start.1 = (f32[112,384]{1,0:T(8,128)S(1)}, f32[112,384]{1,0:T(8,128)S(1)}, u32[]{:S(2)}, u32[]{:S(2)}) collective-permute-start(f32[112,384]{1,0:T(8,128)S(1)} %get-tuple-element.104), channel_id=1, source_target_pairs={{0,4},{2,6},{4,0},{6,2},{1,5},{3,7},{5,1},{7,3},{8,12},{10,14},{12... | collective-permute-start | bytes 516104 | tf_op jit(solution)/shard_map/ppermute | solution.py:343
  12.1 1.5 %collective-permute-start.13 = (f32[72,384]{1,0:T(8,128)S(1)}, f32[72,384]{1,0:T(8,128)S(1)}, u32[]{:S(2)}, u32[]{:S(2)}) collective-permute-start(f32[72,384]{1,0:T(8,128)S(1)} %get-tuple-element.118), channel_id=1, source_target_pairs={{0,16},{1,17},{8,24},{9,25},{16,0},{17,1},{24,8},{25,9},{2,18},{3,... | collective-permute-start | bytes 331784 | tf_op jit(solution)/shard_map/ppermute | solution.py:343
  13.6 1.5 %collective-permute-start.14 = (f32[72,384]{1,0:T(8,128)S(1)}, f32[72,384]{1,0:T(8,128)S(1)}, u32[]{:S(2)}, u32[]{:S(2)}) collective-permute-start(f32[72,384]{1,0:T(8,128)S(1)} %get-tuple-element.119), channel_id=1, source_target_pairs={{0,17},{1,16},{8,25},{9,24},{16,1},{17,0},{24,9},{25,8},{2,19},{3,... | collective-permute-start | bytes 331784 | tf_op jit(solution)/shard_map/ppermute | solution.py:343
  15.1 9.0 %collective-permute-done.1.refs_2_ = f32[112,384]{1,0:T(8,128)S(1)} collective-permute-done((f32[112,384]{1,0:T(8,128)S(1)}, f32[112,384]{1,0:T(8,128)S(1)}, u32[]{:S(2)}, u32[]{:S(2)}) %collective-permute-start.1) | collective-permute-done | bytes 172064 | tf_op jit(solution)/shard_map/ppermute | solution.py:343
  24.8 1.2 %collective-permute-start.16 = (f32[72,384]{1,0:T(8,128)S(1)}, f32[72,384]{1,0:T(8,128)S(1)}, u32[]{:S(2)}, u32[]{:S(2)}) collective-permute-start(f32[72,384]{1,0:T(8,128)S(1)} %get-tuple-element.121), channel_id=1, source_target_pairs={{0,25},{1,24},{8,17},{9,16},{16,9},{17,8},{24,1},{25,0},{2,27},{3,... | collective-permute-start | bytes 331784 | tf_op jit(solution)/shard_map/ppermute | solution.py:343
  26.1 1.1 %shard_map.50 = (f32[80,384]{1,0:T(8,128)S(1)}, f32[80,384]{1,0:T(8,128)S(1)}, f32[80,384]{1,0:T(8,128)S(1)}, f32[80,384]{1,0:T(8,128)S(1)}, f32[80,384]{1,0:T(8...) custom-call(s32[1]{0:T(128)} %bitcast.7.my_ref, ...), custom_call_target="tpu_custom_call" | custom-call | flops 21000000 | bytes 1048576 | tf_op jit(solution)/shard_map/pallas_call | solution.py:371
  27.1 1.3 %collective-permute-start.3 = (f32[80,384]{1,0:T(8,128)S(1)}, f32[80,384]{1,0:T(8,128)S(1)}, u32[]{:S(2)}, u32[]{:S(2)}) collective-permute-start(f32[80,384]{1,0:T(8,128)S(1)} %get-tuple-element.107), channel_id=1, source_target_pairs={{0,1},{1,0},{8,9},{9,8},{16,17},{17,16},{24,25},{25,24},{2,3},{3,2... | collective-permute-start | bytes 368648 | tf_op jit(solution)/shard_map/ppermute | solution.py:343
  28.5 0.9 %collective-permute-start.5 = (f32[80,384]{1,0:T(8,128)S(1)}, f32[80,384]{1,0:T(8,128)S(1)}, u32[]{:S(2)}, u32[]{:S(2)}) collective-permute-start(f32[80,384]{1,0:T(8,128)S(1)} %get-tuple-element.109), channel_id=1, source_target_pairs={{0,9},{1,8},{8,1},{9,0},{16,25},{17,24},{24,17},{25,16},{2,11},{3,... | collective-permute-start | bytes 368648 | tf_op jit(solution)/shard_map/ppermute | solution.py:343
  29.4 1.5 %collective-permute-start.6 = (f32[80,384]{1,0:T(8,128)S(1)}, f32[80,384]{1,0:T(8,128)S(1)}, u32[]{:S(2)}, u32[]{:S(2)}) collective-permute-start(f32[80,384]{1,0:T(8,128)S(1)} %get-tuple-element.110), channel_id=1, source_target_pairs={{0,16},{1,17},{8,24},{9,25},{16,0},{17,1},{24,8},{25,9},{2,18},{3,... | collective-permute-start | bytes 368648 | tf_op jit(solution)/shard_map/ppermute | solution.py:343
  30.9 1.1 %collective-permute-done.16.refs_7_ = f32[72,384]{1,0:T(8,128)S(1)} collective-permute-done((f32[72,384]{1,0:T(8,128)S(1)}, f32[72,384]{1,0:T(8,128)S(1)}, u32[]{:S(2)}, u32[]{:S(2)}) %collective-permute-start.16) | collective-permute-done | bytes 110624 | tf_op jit(solution)/shard_map/ppermute | solution.py:343
  32.0 2.1 %collective-permute-start.7 = (f32[80,384]{1,0:T(8,128)S(1)}, f32[80,384]{1,0:T(8,128)S(1)}, u32[]{:S(2)}, u32[]{:S(2)}) collective-permute-start(f32[80,384]{1,0:T(8,128)S(1)} %get-tuple-element.111), channel_id=1, source_target_pairs={{0,17},{1,16},{8,25},{9,24},{16,1},{17,0},{24,9},{25,8},{2,19},{3,... | collective-permute-start | bytes 368648 | tf_op jit(solution)/shard_map/ppermute | solution.py:343
  34.1 1.1 %shard_map.51 = (f32[128,384]{1,0:T(8,128)S(1)}, f32[128,384]{1,0:T(8,128)S(1)}, f32[128,384]{1,0:T(8,128)S(1)}, f32[128,384]{1,0:T(8,128)S(1)}) custom-call(s32[1]{0:T(128)} %bitcast.7.my_ref, f32[72,384]{1,0:T(8,128)S(1)} %get-tuple-element.114.refs_0_, f32[72,384]{1,0:T(8,128)S(1)} %collective-permute-done.10.refs_1_, ...), custom_call_target="tpu_custom_call" | custom-call | flops 21000000 | bytes 1048576 | tf_op jit(solution)/shard_map/pallas_call | solution.py:371
  35.3 1.7 %collective-permute-start.17 = (f32[128,384]{1,0:T(8,128)S(1)}, f32[128,384]{1,0:T(8,128)S(1)}, u32[]{:S(2)}, u32[]{:S(2)}) collective-permute-start(f32[128,384]{1,0:T(8,128)S(1)} %get-tuple-element.123), channel_id=1, source_target_pairs={{0,2},{2,0},{4,6},{6,4},{1,3},{3,1},{5,7},{7,5},{8,10},{10,8},{12,... | collective-permute-start | bytes 589832 | tf_op jit(solution)/shard_map/ppermute | solution.py:343
  37.0 1.2 %collective-permute-start.18 = (f32[128,384]{1,0:T(8,128)S(1)}, f32[128,384]{1,0:T(8,128)S(1)}, u32[]{:S(2)}, u32[]{:S(2)}) collective-permute-start(f32[128,384]{1,0:T(8,128)S(1)} %get-tuple-element.124), channel_id=1, source_target_pairs={{0,4},{2,6},{4,0},{6,2},{1,5},{3,7},{5,1},{7,3},{8,12},{10,14},{12... | collective-permute-start | bytes 589832 | tf_op jit(solution)/shard_map/ppermute | solution.py:343
  38.2 1.5 %collective-permute-done.5.refs_3_ = f32[80,384]{1,0:T(8,128)S(1)} collective-permute-done((f32[80,384]{1,0:T(8,128)S(1)}, f32[80,384]{1,0:T(8,128)S(1)}, u32[]{:S(2)}, u32[]{:S(2)}) %collective-permute-start.5) | collective-permute-done | bytes 122912 | tf_op jit(solution)/shard_map/ppermute | solution.py:343
  39.8 2.6 %collective-permute-start.19 = (f32[128,384]{1,0:T(8,128)S(1)}, f32[128,384]{1,0:T(8,128)S(1)}, u32[]{:S(2)}, u32[]{:S(2)}) collective-permute-start(f32[128,384]{1,0:T(8,128)S(1)} %get-tuple-element.125), channel_id=1, source_target_pairs={{0,6},{2,4},{4,2},{6,0},{1,7},{3,5},{5,3},{7,1},{8,14},{10,12},{12... | collective-permute-start | bytes 589832 | tf_op jit(solution)/shard_map/ppermute | solution.py:343
  42.7 2.3 %collective-permute-start.9 = (f32[80,384]{1,0:T(8,128)S(1)}, f32[80,384]{1,0:T(8,128)S(1)}, u32[]{:S(2)}, u32[]{:S(2)}) collective-permute-start(f32[80,384]{1,0:T(8,128)S(1)} %get-tuple-element.113), channel_id=1, source_target_pairs={{0,25},{1,24},{8,17},{9,16},{16,9},{17,8},{24,1},{25,0},{2,27},{3,... | collective-permute-start | bytes 368648 | tf_op jit(solution)/shard_map/ppermute | solution.py:343
  45.0 2.9 %collective-permute-done.8.refs_6_ = f32[80,384]{1,0:T(8,128)S(1)} collective-permute-done((f32[80,384]{1,0:T(8,128)S(1)}, f32[80,384]{1,0:T(8,128)S(1)}, u32[]{:S(2)}, u32[]{:S(2)}) %collective-permute-start.8) | collective-permute-done | bytes 122912 | tf_op jit(solution)/shard_map/ppermute | solution.py:343
  47.9 3.5 %collective-permute-done.9.refs_7_ = f32[80,384]{1,0:T(8,128)S(1)} collective-permute-done((f32[80,384]{1,0:T(8,128)S(1)}, f32[80,384]{1,0:T(8,128)S(1)}, u32[]{:S(2)}, u32[]{:S(2)}) %collective-permute-start.9) | collective-permute-done | bytes 122912 | tf_op jit(solution)/shard_map/ppermute | solution.py:343
  51.4 2.3 %collective-permute-done.18.refs_10_ = f32[128,384]{1,0:T(8,128)S(1)} collective-permute-done((f32[128,384]{1,0:T(8,128)S(1)}, f32[128,384]{1,0:T(8,128)S(1)}, u32[]{:S(2)}, u32[]{:S(2)}) %collective-permute-start.18) | collective-permute-done | bytes 196640 | tf_op jit(solution)/shard_map/ppermute | solution.py:343
  53.7 5.3 %finish.1 = (f32[1024,768]{1,0:T(8,128)}, f32[1024,768]{1,0:T(8,128)}, s32[1,1]{1,0:T(1,128)}) custom-call(s32[1]{0:T(128)} %bitcast.7.my_ref, f32[80,384]{1,0:T(8,128)S(1)} %get-tuple-element.106.refs_0_, f32[80,384]{1,0:T(8,128)S(1)} %collective-permute-done.3.refs_1_, f32[80,384]{1,0:T(8,128)S(1)} %collective-permute-done.4.refs_2_, ...), custom_call_target="tpu_custom_call" | custom-call | flops 42000000 | bytes 1048576 | tf_op jit(solution)/shard_map/finish/pallas_call | solution.py:385
  (27 shorter events, 2.7 us)
Async XLA Ops:
  0.6 58.4 %copy-start = (f32[512,768]{1,0:T(8,128)S(1)}, f32[512,768]{1,0:T(8,128)}, u32[]{:S(2)}) copy-start(f32[512,768]{1,0:T(8,128)} %points_ref.1) | copy-start | bytes 4718596
  0.6 58.4 %copy-start.2 = (s32[512]{0:T(512)S(1)}, s32[512]{0:T(512)}, u32[]{:S(2)}) copy-start(s32[512]{0:T(512)} %param.8) | copy-start | bytes 6148
  0.6 58.4 %copy-start.3 = (s32[512]{0:T(512)S(1)}, s32[512]{0:T(512)}, u32[]{:S(2)}) copy-start(s32[512]{0:T(512)} %param.9) | copy-start | bytes 6148
  4.2 9.4 %collective-permute-start = (f32[112,384]{1,0:T(8,128)S(1)}, f32[112,384]{1,0:T(8,128)S(1)}, u32[]{:S(2)}, u32[]{:S(2)}) collective-permute-start(f32[112,384]{1,0:T(8,128)S(1)} %get-tuple-element.103), channel_id=1, source_target_pairs={{0,2},{2,0},{4,6},{6,4},{1,3},{3,1},{5,7},{7,5},{8,10},{10,8},{12,... | collective-permute-start | bytes 516104 | tf_op jit(solution)/shard_map/ppermute | solution.py:343
  7.3 4.7 %collective-permute-start.10 = (f32[72,384]{1,0:T(8,128)S(1)}, f32[72,384]{1,0:T(8,128)S(1)}, u32[]{:S(2)}, u32[]{:S(2)}) collective-permute-start(f32[72,384]{1,0:T(8,128)S(1)} %get-tuple-element.115), channel_id=1, source_target_pairs={{0,1},{1,0},{8,9},{9,8},{16,17},{17,16},{24,25},{25,24},{2,3},{3,2... | collective-permute-start | bytes 331784 | tf_op jit(solution)/shard_map/ppermute | solution.py:343
  8.8 3.2 %collective-permute-start.11 = (f32[72,384]{1,0:T(8,128)S(1)}, f32[72,384]{1,0:T(8,128)S(1)}, u32[]{:S(2)}, u32[]{:S(2)}) collective-permute-start(f32[72,384]{1,0:T(8,128)S(1)} %get-tuple-element.116), channel_id=1, source_target_pairs={{0,8},{1,9},{8,0},{9,1},{16,24},{17,25},{24,16},{25,17},{2,10},{3,... | collective-permute-start | bytes 331784 | tf_op jit(solution)/shard_map/ppermute | solution.py:343
  8.8 15.2 %collective-permute-start.1 = (f32[112,384]{1,0:T(8,128)S(1)}, f32[112,384]{1,0:T(8,128)S(1)}, u32[]{:S(2)}, u32[]{:S(2)}) collective-permute-start(f32[112,384]{1,0:T(8,128)S(1)} %get-tuple-element.104), channel_id=1, source_target_pairs={{0,4},{2,6},{4,0},{6,2},{1,5},{3,7},{5,1},{7,3},{8,12},{10,14},{12... | collective-permute-start | bytes 516104 | tf_op jit(solution)/shard_map/ppermute | solution.py:343
  11.4 13.4 %collective-permute-start.2 = (f32[112,384]{1,0:T(8,128)S(1)}, f32[112,384]{1,0:T(8,128)S(1)}, u32[]{:S(2)}, u32[]{:S(2)}) collective-permute-start(f32[112,384]{1,0:T(8,128)S(1)} %get-tuple-element.105), channel_id=1, source_target_pairs={{0,6},{2,4},{4,2},{6,0},{1,7},{3,5},{5,3},{7,1},{8,14},{10,12},{12... | collective-permute-start | bytes 516104 | tf_op jit(solution)/shard_map/ppermute | solution.py:343
  12.1 15.1 %collective-permute-start.12 = (f32[72,384]{1,0:T(8,128)S(1)}, f32[72,384]{1,0:T(8,128)S(1)}, u32[]{:S(2)}, u32[]{:S(2)}) collective-permute-start(f32[72,384]{1,0:T(8,128)S(1)} %get-tuple-element.117), channel_id=1, source_target_pairs={{0,9},{1,8},{8,1},{9,0},{16,25},{17,24},{24,17},{25,16},{2,11},{3,... | collective-permute-start | bytes 331784 | tf_op jit(solution)/shard_map/ppermute | solution.py:343
  12.1 16.4 %collective-permute-start.13 = (f32[72,384]{1,0:T(8,128)S(1)}, f32[72,384]{1,0:T(8,128)S(1)}, u32[]{:S(2)}, u32[]{:S(2)}) collective-permute-start(f32[72,384]{1,0:T(8,128)S(1)} %get-tuple-element.118), channel_id=1, source_target_pairs={{0,16},{1,17},{8,24},{9,25},{16,0},{17,1},{24,8},{25,9},{2,18},{3,... | collective-permute-start | bytes 331784 | tf_op jit(solution)/shard_map/ppermute | solution.py:343
  13.6 14.9 %collective-permute-start.14 = (f32[72,384]{1,0:T(8,128)S(1)}, f32[72,384]{1,0:T(8,128)S(1)}, u32[]{:S(2)}, u32[]{:S(2)}) collective-permute-start(f32[72,384]{1,0:T(8,128)S(1)} %get-tuple-element.119), channel_id=1, source_target_pairs={{0,17},{1,16},{8,25},{9,24},{16,1},{17,0},{24,9},{25,8},{2,19},{3,... | collective-permute-start | bytes 331784 | tf_op jit(solution)/shard_map/ppermute | solution.py:343
  24.1 5.3 %collective-permute-start.15 = (f32[72,384]{1,0:T(8,128)S(1)}, f32[72,384]{1,0:T(8,128)S(1)}, u32[]{:S(2)}, u32[]{:S(2)}) collective-permute-start(f32[72,384]{1,0:T(8,128)S(1)} %get-tuple-element.120), channel_id=1, source_target_pairs={{0,24},{1,25},{8,16},{9,17},{16,8},{17,9},{24,0},{25,1},{2,26},{3,... | collective-permute-start | bytes 331784 | tf_op jit(solution)/shard_map/ppermute | solution.py:343
  24.8 7.2 %collective-permute-start.16 = (f32[72,384]{1,0:T(8,128)S(1)}, f32[72,384]{1,0:T(8,128)S(1)}, u32[]{:S(2)}, u32[]{:S(2)}) collective-permute-start(f32[72,384]{1,0:T(8,128)S(1)} %get-tuple-element.121), channel_id=1, source_target_pairs={{0,25},{1,24},{8,17},{9,16},{16,9},{17,8},{24,1},{25,0},{2,27},{3,... | collective-permute-start | bytes 331784 | tf_op jit(solution)/shard_map/ppermute | solution.py:343
  27.1 8.1 %collective-permute-start.3 = (f32[80,384]{1,0:T(8,128)S(1)}, f32[80,384]{1,0:T(8,128)S(1)}, u32[]{:S(2)}, u32[]{:S(2)}) collective-permute-start(f32[80,384]{1,0:T(8,128)S(1)} %get-tuple-element.107), channel_id=1, source_target_pairs={{0,1},{1,0},{8,9},{9,8},{16,17},{17,16},{24,25},{25,24},{2,3},{3,2... | collective-permute-start | bytes 368648 | tf_op jit(solution)/shard_map/ppermute | solution.py:343
  28.4 8.6 %collective-permute-start.4 = (f32[80,384]{1,0:T(8,128)S(1)}, f32[80,384]{1,0:T(8,128)S(1)}, u32[]{:S(2)}, u32[]{:S(2)}) collective-permute-start(f32[80,384]{1,0:T(8,128)S(1)} %get-tuple-element.108), channel_id=1, source_target_pairs={{0,8},{1,9},{8,0},{9,1},{16,24},{17,25},{24,16},{25,17},{2,10},{3,... | collective-permute-start | bytes 368648 | tf_op jit(solution)/shard_map/ppermute | solution.py:343
  28.5 11.3 %collective-permute-start.5 = (f32[80,384]{1,0:T(8,128)S(1)}, f32[80,384]{1,0:T(8,128)S(1)}, u32[]{:S(2)}, u32[]{:S(2)}) collective-permute-start(f32[80,384]{1,0:T(8,128)S(1)} %get-tuple-element.109), channel_id=1, source_target_pairs={{0,9},{1,8},{8,1},{9,0},{16,25},{17,24},{24,17},{25,16},{2,11},{3,... | collective-permute-start | bytes 368648 | tf_op jit(solution)/shard_map/ppermute | solution.py:343
  29.4 13.0 %collective-permute-start.6 = (f32[80,384]{1,0:T(8,128)S(1)}, f32[80,384]{1,0:T(8,128)S(1)}, u32[]{:S(2)}, u32[]{:S(2)}) collective-permute-start(f32[80,384]{1,0:T(8,128)S(1)} %get-tuple-element.110), channel_id=1, source_target_pairs={{0,16},{1,17},{8,24},{9,25},{16,0},{17,1},{24,8},{25,9},{2,18},{3,... | collective-permute-start | bytes 368648 | tf_op jit(solution)/shard_map/ppermute | solution.py:343
  32.0 10.7 %collective-permute-start.7 = (f32[80,384]{1,0:T(8,128)S(1)}, f32[80,384]{1,0:T(8,128)S(1)}, u32[]{:S(2)}, u32[]{:S(2)}) collective-permute-start(f32[80,384]{1,0:T(8,128)S(1)} %get-tuple-element.111), channel_id=1, source_target_pairs={{0,17},{1,16},{8,25},{9,24},{16,1},{17,0},{24,9},{25,8},{2,19},{3,... | collective-permute-start | bytes 368648 | tf_op jit(solution)/shard_map/ppermute | solution.py:343
  35.3 16.1 %collective-permute-start.17 = (f32[128,384]{1,0:T(8,128)S(1)}, f32[128,384]{1,0:T(8,128)S(1)}, u32[]{:S(2)}, u32[]{:S(2)}) collective-permute-start(f32[128,384]{1,0:T(8,128)S(1)} %get-tuple-element.123), channel_id=1, source_target_pairs={{0,2},{2,0},{4,6},{6,4},{1,3},{3,1},{5,7},{7,5},{8,10},{10,8},{12,... | collective-permute-start | bytes 589832 | tf_op jit(solution)/shard_map/ppermute | solution.py:343
  37.0 16.7 %collective-permute-start.18 = (f32[128,384]{1,0:T(8,128)S(1)}, f32[128,384]{1,0:T(8,128)S(1)}, u32[]{:S(2)}, u32[]{:S(2)}) collective-permute-start(f32[128,384]{1,0:T(8,128)S(1)} %get-tuple-element.124), channel_id=1, source_target_pairs={{0,4},{2,6},{4,0},{6,2},{1,5},{3,7},{5,1},{7,3},{8,12},{10,14},{12... | collective-permute-start | bytes 589832 | tf_op jit(solution)/shard_map/ppermute | solution.py:343
  39.8 13.9 %collective-permute-start.19 = (f32[128,384]{1,0:T(8,128)S(1)}, f32[128,384]{1,0:T(8,128)S(1)}, u32[]{:S(2)}, u32[]{:S(2)}) collective-permute-start(f32[128,384]{1,0:T(8,128)S(1)} %get-tuple-element.125), channel_id=1, source_target_pairs={{0,6},{2,4},{4,2},{6,0},{1,7},{3,5},{5,3},{7,1},{8,14},{10,12},{12... | collective-permute-start | bytes 589832 | tf_op jit(solution)/shard_map/ppermute | solution.py:343
  42.3 5.5 %collective-permute-start.8 = (f32[80,384]{1,0:T(8,128)S(1)}, f32[80,384]{1,0:T(8,128)S(1)}, u32[]{:S(2)}, u32[]{:S(2)}) collective-permute-start(f32[80,384]{1,0:T(8,128)S(1)} %get-tuple-element.112), channel_id=1, source_target_pairs={{0,24},{1,25},{8,16},{9,17},{16,8},{17,9},{24,0},{25,1},{2,26},{3,... | collective-permute-start | bytes 368648 | tf_op jit(solution)/shard_map/ppermute | solution.py:343
  42.7 8.7 %collective-permute-start.9 = (f32[80,384]{1,0:T(8,128)S(1)}, f32[80,384]{1,0:T(8,128)S(1)}, u32[]{:S(2)}, u32[]{:S(2)}) collective-permute-start(f32[80,384]{1,0:T(8,128)S(1)} %get-tuple-element.113), channel_id=1, source_target_pairs={{0,25},{1,24},{8,17},{9,16},{16,9},{17,8},{24,1},{25,0},{2,27},{3,... | collective-permute-start | bytes 368648 | tf_op jit(solution)/shard_map/ppermute | solution.py:343
